TPU v7x, 32 devices: a whole 2x2x4 slice. The times are simulated.
32 devices in a mesh: dp: 4 (over x, core), mp: 8 (over z, y).
Axes of the slice: x: 2, y: 2, z: 4, core: 2. Of those that a mesh axis runs over, the one named last changes fastest.
Arguments:
- source_prompts: bfloat16 [128, 64, 4096], P(None, None, 'mp'), may hold values from -6 to 6
- task_logits: float32 [8, 128], replicated, may hold values from -8 to 260
- task_ids: int32 [32], P('dp'), may hold values from 0 to 7
- key_weight: bfloat16 [4096, 4096], P(None, 'mp'), may hold values from -0.09375 to 0.09375
- value_weight: bfloat16 [4096, 4096], P(None, 'mp'), may hold values from -0.09375 to 0.09375
- queries: bfloat16 [32, 128, 4096], P(('dp', 'mp')), may hold values from -32 to 32
- keys: bfloat16 [32, 128, 4096], P(('dp', 'mp')), may hold values from -16 to 16
- values: bfloat16 [32, 128, 4096], P(('dp', 'mp')), may hold values from -6 to 6
- cotangent: bfloat16 [32, 128, 4096], P(('dp', 'mp')), may hold values from -6 to 6
Outputs:
- attended: bfloat16 [32, 128, 4096], P(('dp', 'mp'))
- source_grad: float32 [128, 64, 4096], P(None, 'dp', 'mp')
- logits_grad: float32 [8, 128], replicated
All inputs are finite; a program needn't handle non-finite values.
Results may differ from a plain program's by a relative error of at most 0.011.
Values may be sent and summed in bfloat16 or wider, within the bound.
A program may use at most 128 MiB of HBM per device.

v0:
```python
import functools

import jax
import jax.numpy as jnp
from jax import lax
from jax.experimental import pallas as pl
from jax.experimental.pallas import tpu as pltpu
from jax.sharding import PartitionSpec as P

D = 4096
HEADS = 32
DH = 128
NSRC = 128
NTASK = 8
PTOK = 64
SEQ = 128
E_DEV = 1


mask_fill = -1e30


def example_block(prompt_pair, queries, keys, values, cotangent):
    examples = queries.shape[0]
    score_scale = DH ** (-0.5)
    key_all = jnp.concatenate([prompt_pair[:, :, 0, :], keys], axis=1)
    value_all = jnp.concatenate([prompt_pair[:, :, 1, :], values], axis=1)
    query_heads = queries.reshape(examples, SEQ, HEADS, DH)
    key_heads = key_all.reshape(examples, PTOK + SEQ, HEADS, DH)
    value_heads = value_all.reshape(examples, PTOK + SEQ, HEADS, DH)
    cot_heads = cotangent.reshape(examples, SEQ, HEADS, DH)
    scores = (
        jnp.einsum("eihd,ejhd->ehij", query_heads, key_heads, preferred_element_type=jnp.float32)
        * score_scale
    )
    column = jnp.arange(PTOK + SEQ)[None, :]
    position = jnp.arange(SEQ)[:, None]
    visible = (column < PTOK) | (column - PTOK <= position)
    scores = jnp.where(visible[None, None], scores, mask_fill)
    top_score = jnp.max(scores, axis=3, keepdims=True)
    exponent = jnp.exp(scores - top_score)
    attention = exponent / jnp.sum(exponent, axis=3, keepdims=True)
    attention_rounded = attention.astype(jnp.bfloat16)
    attended = jnp.einsum(
        "ehij,ejhd->eihd", attention_rounded, value_heads, preferred_element_type=jnp.float32
    )
    attended = attended.astype(jnp.bfloat16).reshape(examples, SEQ, D)
    grad_attention = jnp.einsum(
        "eihd,ejhd->ehij", cot_heads, value_heads, preferred_element_type=jnp.float32
    )
    inner_sum = jnp.sum(attention * grad_attention, axis=3, keepdims=True)
    grad_scores = (attention * (grad_attention - inner_sum)).astype(jnp.bfloat16)
    key_grads = jnp.einsum(
        "ehij,eihd->ejhd",
        grad_scores[:, :, :, :PTOK],
        query_heads,
        preferred_element_type=jnp.float32,
    )
    key_grads = (key_grads * score_scale).astype(jnp.bfloat16).reshape(examples, PTOK, D)
    value_grads = jnp.einsum(
        "ehij,eihd->ejhd",
        attention_rounded[:, :, :, :PTOK],
        cot_heads,
        preferred_element_type=jnp.float32,
    )
    value_grads = value_grads.astype(jnp.bfloat16).reshape(examples, PTOK, D)
    return (attended, jnp.stack([key_grads, value_grads], axis=2))


def tile_products(tile_grad, source_prompts, mix_weights, col_width):
    rows_here = tile_grad.shape[1]
    own_prompts = lax.dynamic_slice_in_dim(
        source_prompts, lax.axis_index("dp") * rows_here, rows_here, 1
    )
    tile_flat = tile_grad.reshape(NTASK, rows_here * col_width)
    source_grad = jnp.dot(mix_weights.T, tile_flat, precision=lax.Precision.HIGHEST)
    source_grad = source_grad.reshape(NSRC, rows_here, col_width)
    weight_part = jnp.dot(
        tile_flat,
        own_prompts.reshape(NSRC, rows_here * col_width).astype(jnp.float32).T,
        precision=lax.Precision.HIGHEST,
    )
    return (source_grad, weight_part)


def on_device(
    source_prompts,
    task_logits,
    task_ids,
    key_weight,
    value_weight,
    queries,
    keys,
    values,
    cotangent,
):
    col_width = key_weight.shape[1]
    group_examples = task_ids.shape[0]
    mix_weights = jax.nn.softmax(task_logits, axis=1)
    mix_rounded = mix_weights.astype(jnp.bfloat16)
    mixture = jnp.dot(
        mix_rounded,
        source_prompts.reshape(NSRC, PTOK * col_width),
        preferred_element_type=jnp.float32,
    )
    mixture = mixture.astype(jnp.bfloat16).reshape(NTASK, PTOK, col_width)
    pair_weight = jnp.concatenate([key_weight, value_weight], axis=1)
    portion = lax.all_gather(mixture, "mp", axis=2, tiled=True)
    portion_rows = portion.reshape(NTASK * PTOK, portion.shape[2])
    projected = jnp.dot(portion_rows, pair_weight, preferred_element_type=jnp.float32)
    projected = projected.astype(jnp.bfloat16).reshape(NTASK, PTOK, 2, col_width)
    task_range = jnp.arange(NTASK, dtype=jnp.int32)
    selector_all = (task_ids[:, None] == task_range[None, :]).astype(jnp.bfloat16)
    table_full = lax.all_gather(projected, "mp", axis=3, tiled=True)
    own_offset = lax.axis_index("mp") * E_DEV
    own_selector = lax.dynamic_slice_in_dim(selector_all, own_offset, E_DEV, 0)
    chosen = jnp.dot(
        own_selector, table_full.reshape(NTASK, PTOK * 2 * D), preferred_element_type=jnp.float32
    )
    prompt_pair = chosen.astype(jnp.bfloat16).reshape(E_DEV, PTOK, 2, D)
    attended, outgoing_grads = example_block(prompt_pair, queries, keys, values, cotangent)
    incoming = lax.all_to_all(outgoing_grads, "mp", split_axis=3, concat_axis=0, tiled=True)
    group_grads = jnp.dot(
        selector_all.T,
        incoming.reshape(group_examples, PTOK * 2 * col_width),
        preferred_element_type=jnp.float32,
    )
    pair_weight_t = pair_weight.astype(jnp.float32).T
    task_rows = lax.psum_scatter(
        group_grads.reshape(NTASK, PTOK, 2 * col_width), "dp", scatter_dimension=1, tiled=True
    )
    rows_here = task_rows.shape[1]
    row_terms = jnp.dot(
        task_rows.reshape(NTASK * rows_here, 2 * col_width),
        pair_weight_t,
        precision=lax.Precision.HIGHEST,
    ).reshape(NTASK, rows_here, D)
    tile_grad = lax.psum_scatter(row_terms, "mp", scatter_dimension=2, tiled=True)
    source_grad, weight_part = tile_products(tile_grad, source_prompts, mix_weights, col_width)
    weight_grad = lax.psum(weight_part, ("dp", "mp"))
    logits_grad = mix_weights * (
        weight_grad - jnp.sum(mix_weights * weight_grad, axis=1, keepdims=True)
    )
    return (attended, source_grad, logits_grad)


BF = jnp.bfloat16
F32 = jnp.float32


def mm(a, b, ca=1, cb=0, precision=None):
    return lax.dot_general(
        a, b, (((ca,), (cb,)), ((), ())), preferred_element_type=F32, precision=precision
    )


def chain_kernel(
    ndp, nmp,
    logits, ids_in, sp_hbm, kw_hbm, vw_hbm, q_hbm, k_hbm, v_hbm, c_hbm,
    att_hbm, tile_out, lg_out, w_hbm,
    att_out, w_out, p_v, kw_v, vw_v, q_v, k_v, v_v, c_v,
    mixed, ids_own, ids_buf, sbuf, pair, gr, rbuf, ys, yr, zs, zr, wp, wbuf,
    lsem, gs, gv, fs, fv, js, jv, bs, bv, cs, cv, us, uv, ts, tv, ws, wv,
):
    n = ndp * nmp
    nz = nmp // 2
    width = kw_v.shape[1]
    rows = p_v.shape[1]
    nsrc = p_v.shape[0]
    ntask = logits.shape[0]
    tp = ntask * rows
    spn = nsrc * rows
    seq = q_v.shape[0]
    d = lax.axis_index("dp")
    m = lax.axis_index("mp")
    z = m // 2
    y = m % 2
    me = d * nmp + m
    other = z * 2 + (1 - y)

    shift = rows.bit_length() - 1

    def iota(shape, axis):
        return lax.broadcasted_iota(jnp.int32, shape, axis)

    def outer(a):
        return lax.shift_right_logical(a, jnp.int32(shift))

    def same_row(shape):
        return ((iota(shape, 0) ^ iota(shape, 1)) & (rows - 1)) == 0

    def remote(src, dst, ss, rs, dd, mm_):
        return pltpu.make_async_remote_copy(
            src_ref=src, dst_ref=dst, send_sem=ss, recv_sem=rs,
            device_id=(dd, mm_), device_id_type=pl.DeviceIdType.MESH,
        )

    barrier = pltpu.get_barrier_semaphore()

    @pl.loop(1, n)
    def _(k):
        to = lax.rem(me + k, n)
        pl.semaphore_signal(
            barrier, inc=1, device_id=(to // nmp, lax.rem(to, nmp)),
            device_id_type=pl.DeviceIdType.MESH,
        )

    loads = [
        pltpu.make_async_copy(
            sp_hbm.at[:, pl.ds(pl.multiple_of(d * rows, rows), rows), :], p_v, lsem.at[0]
        )
    ]
    for i, (a, b) in enumerate(
        ((kw_hbm, kw_v), (vw_hbm, vw_v), (k_hbm, k_v), (q_hbm, q_v), (v_hbm, v_v), (c_hbm, c_v))
    ):
        loads.append(pltpu.make_async_copy(a, b, lsem.at[1 + i]))
    loads[0].start()

    lg = logits[...]
    ex = jnp.exp(lg - jnp.max(lg, axis=1, keepdims=True))
    mix = ex / jnp.sum(ex, axis=1, keepdims=True)
    up = (
        outer(iota((tp, ntask), 0)) == iota((tp, ntask), 1)
    )
    tall = mm(jnp.where(up, 1.0, 0.0), mix.astype(BF).astype(F32)).astype(BF)
    out = (
        outer(iota((nsrc, spn), 1)) == iota((nsrc, spn), 0)
    )
    wide = mm(tall, jnp.where(out, 1.0, 0.0).astype(BF))
    w_out[...] = jnp.where(same_row((tp, spn)), wide, 0.0).astype(BF)
    for j in range(ids_in.shape[0]):
        line = jnp.full((1, tp), ids_in[j], jnp.int32).astype(F32)
        ids_own[pl.ds(j, 1), :] = line
        ids_buf[d, pl.ds(j, 1), :] = line

    loads[0].wait()
    for c in loads[1:]:
        c.start()
    w_save = pltpu.make_async_copy(w_out, w_hbm, lsem.at[9])
    w_save.start()
    mixed[m] = mm(w_out[...], p_v[...].reshape(spn, width)).astype(BF)

    pl.semaphore_wait(barrier, n - 1)

    idc = []
    for j in range(1, ndp):
        c = remote(ids_own, ids_buf.at[d], js.at[j], jv.at[j], lax.rem(d + j, ndp), m)
        c.start()
        idc.append(c)
    gat = []
    for j in range(1, nz):
        c = remote(
            mixed.at[m], mixed.at[m], gs.at[j], gv.at[j], d, lax.rem(z + j, nz) * 2 + y
        )
        c.start()
        gat.append(c)
    fwd = [remote(mixed.at[m], mixed.at[m], fs.at[0], fv.at[0], d, other)]
    fwd[0].start()
    for c in idc:
        c.wait()
    loads[1].wait()
    loads[2].wait()

    def part(slot):
        block = mixed[slot]
        at = pl.ds(pl.multiple_of(slot * width, width), width)
        return mm(block, kw_v[at, :]), mm(block, vw_v[at, :])

    pk, pv = part(m)
    for j in range(1, nz):
        slot = lax.rem(z + nz - j, nz) * 2 + y
        gat[j - 1].wait_recv()
        c = remote(mixed.at[slot], mixed.at[slot], fs.at[j], fv.at[j], d, other)
        c.start()
        fwd.append(c)
        a, b = part(slot)
        pk, pv = pk + a, pv + b
    for j in range(nz):
        slot = lax.rem(z + nz - j, nz) * 2 + (1 - y)
        fwd[j].wait_recv()
        a, b = part(slot)
        pk, pv = pk + a, pv + b

    ids_all = ids_buf[...].reshape(n, tp).astype(BF)
    rep = (
        outer(iota((n * rows, n), 0)) == iota((n * rows, n), 1)
    )
    ids_x = mm(jnp.where(rep, 1.0, 0.0).astype(BF), ids_all)
    sel = jnp.where(
        (ids_x == outer(iota((n * rows, tp), 1)).astype(F32)) & same_row((n * rows, tp)), 1.0, 0.0
    ).astype(BF)
    sbuf[:, 0] = mm(sel, pk.astype(BF)).astype(BF).reshape(n, rows, width)
    sbuf[:, 1] = mm(sel, pv.astype(BF)).astype(BF).reshape(n, rows, width)

    my_rows = pl.ds(pl.multiple_of(d * rows, rows), rows)
    my_cols = pl.ds(pl.multiple_of(m * width, width), width)

    def b_copy(k):
        dd, gg = lax.rem(k, ndp), k // ndp
        td, tm = lax.rem(d + ndp - dd, ndp), lax.rem(m + nmp - gg, nmp)
        return remote(
            sbuf.at[td * nmp + tm], pair.at[:, my_rows, my_cols], bs.at[k], bv.at[k], td, tm
        )

    own_b = pltpu.make_async_copy(sbuf.at[me], pair.at[:, my_rows, my_cols], lsem.at[7])
    own_b.start()

    def turn(t):
        return lax.rem(t + nmp // 2 - 1 + t // (nmp // 2 + 1), nmp)

    @pl.loop(1, nmp)
    def _(t):
        @pl.loop(0, ndp)
        def _(dd):
            b_copy(turn(t) * ndp + dd).start()

    @pl.loop(1, ndp)
    def _(dd):
        b_copy(dd).start()

    for c in loads[3:]:
        c.wait()
    own_b.wait()

    def c_copy(k):
        dd, gg = lax.rem(k, ndp), k // ndp
        td, tm = lax.rem(d + dd, ndp), lax.rem(m + gg, nmp)
        return remote(
            gr.at[
                :,
                pl.ds(pl.multiple_of(td * rows, rows), rows),
                pl.ds(pl.multiple_of(tm * width, width), width),
            ],
            rbuf.at[me], cs.at[k], cv.at[k], td, tm,
        )

    scale = DH ** (-0.5)
    to_exp2 = scale * 1.4426950408889634
    ptok = pair.shape[1]
    seen = iota((seq, seq), 0) <= iota((seq, seq), 1)

    def group(g, wait_from):
        @pl.loop(wait_from, ndp)
        def _(dd):
            b_copy(g * ndp + dd).wait_recv()

        base = lax.rem(m + g, nmp) * width
        ats, st, gt, va = [], [], [], []
        for h in range(width // DH):
            at = pl.ds(pl.multiple_of(base + h * DH, DH), DH)
            ats.append(at)
            ka = jnp.concatenate([pair[0, :, at], k_v[:, at]], axis=0)
            va.append(jnp.concatenate([pair[1, :, at], v_v[:, at]], axis=0))
            st.append(mm(ka, q_v[:, at], 1, 1))
            gt.append(mm(va[h], c_v[:, at], 1, 1))
        for h in range(width // DH):
            at = ats[h]
            s = st[h] * to_exp2
            s = jnp.concatenate([s[:ptok], jnp.where(seen, s[ptok:], mask_fill)], axis=0)
            e = jnp.exp2(s - jnp.max(s, axis=0, keepdims=True))
            a = e * (1.0 / jnp.sum(e, axis=0, keepdims=True))
            ab = a.astype(BF)
            inner = jnp.sum(a * gt[h], axis=0, keepdims=True)
            gs1 = (a[:ptok] * (gt[h][:ptok] - inner)).astype(BF)
            gr[0, :, at] = (mm(gs1, q_v[:, at]) * scale).astype(BF)
            gr[1, :, at] = mm(ab[:ptok], c_v[:, at]).astype(BF)
            att_out[:, at] = mm(ab, va[h], 0, 0).astype(BF)

    group(0, 1)
    own_c = pltpu.make_async_copy(gr.at[:, my_rows, my_cols], rbuf.at[me], lsem.at[8])
    own_c.start()

    @pl.loop(1, ndp)
    def _(dd):
        c_copy(dd).start()

    @pl.loop(1, nmp)
    def _(t):
        g = turn(t)
        group(g, 0)

        @pl.loop(0, ndp)
        def _(dd):
            c_copy(g * ndp + dd).start()

    own_c.wait()
    att_save = pltpu.make_async_copy(att_out, att_hbm, lsem.at[10])
    att_save.start()

    @pl.loop(1, n)
    def _(k):
        c_copy(k).wait_recv()

    tk = mm(sel, rbuf[:, 0].reshape(n * rows, width), 0, 0).astype(BF)
    tv_ = mm(sel, rbuf[:, 1].reshape(n * rows, width), 0, 0).astype(BF)

    def term(slot):
        at = pl.ds(pl.multiple_of(slot * width, width), width)
        return mm(tk, kw_v[at, :], 1, 1) + mm(tv_, vw_v[at, :], 1, 1)

    yc, zc = [None] * nz, [None] * nz
    order = list(range(1, nz)) + [0]
    for j in order:
        ys[j] = term(lax.rem(z + j, nz) * 2 + (1 - y)).astype(BF)
        yc[j] = remote(ys.at[j], yr.at[j], us.at[j], uv.at[j], d, other)
        yc[j].start()
    for j in order:
        to = lax.rem(z + j, nz) * 2 + y
        mine = term(to)
        yc[j].wait_recv()
        mine = mine + yr[j].astype(F32)
        if j:
            zs[j] = mine.astype(BF)
            zc[j] = remote(zs.at[j], zr.at[j], ts.at[j], tv.at[j], d, to)
            zc[j].start()
    for j in range(1, nz):
        zc[j].wait_recv()
        mine = mine + zr[j].astype(F32)
    tile = mine.astype(BF)
    tile_out[...] = tile

    prod = mm(p_v[...].reshape(spn, width), tile, 1, 1)
    prod = jnp.sum(jnp.where(same_row((spn, tp)), prod, 0.0).reshape(nsrc, rows, tp), axis=1)
    fold = (
        outer(iota((ntask, tp), 1)) == iota((ntask, tp), 0)
    )
    part_w = mm(jnp.where(fold, 1.0, 0.0), prod, 1, 1, lax.Precision.HIGHEST)
    wp[...] = part_w
    wbuf[me] = part_w

    def w_copy(k):
        to = lax.rem(me + k, n)
        return remote(wp, wbuf.at[me], ws.at[k], wv.at[k], to // nmp, lax.rem(to, nmp))

    @pl.loop(1, n)
    def _(k):
        w_copy(k).start()

    w_save.wait()
    att_save.wait()
    for c in gat + fwd + yc + zc[1:]:
        c.wait_send()

    @pl.loop(1, n)
    def _(k):
        b_copy(k).wait_send()
        c_copy(k).wait_send()

    @pl.loop(1, n)
    def _(k):
        w_copy(k).wait()

    wg = jnp.sum(wbuf[...], axis=0)
    lg_out[...] = mix * (wg - jnp.sum(mix * wg, axis=1, keepdims=True))


def source_kernel(w_ref, tile_ref, att_ref, lg_ref, out_ref, att_out, lg_out):
    att_out[...] = att_ref[...]
    lg_out[...] = lg_ref[...]
    got = mm(w_ref[...], tile_ref[...], 0, 0)
    out_ref[...] = got.reshape(out_ref.shape)


def per_device(ndp, nmp, *args):
    source_prompts, task_logits, task_ids, key_weight, value_weight = args[:5]
    queries, keys, values, cotangent = args[5:]
    nsrc, ptok, width = source_prompts.shape
    ntask = task_logits.shape[0]
    ge = task_ids.shape[0]
    rows = ptok // ndp
    if width % DH or nmp % 4 or ge != nmp or ptok % ndp or rows % 16 or rows & (rows - 1) or ntask * rows != 128:
        return on_device(*args)
    n, nz = ndp * nmp, nmp // 2
    tp, spn = ntask * rows, nsrc * rows
    seq, full = queries.shape[1:]
    vmem = pl.BlockSpec(memory_space=pltpu.VMEM)
    hbm = pl.BlockSpec(memory_space=pl.ANY)
    dma = pltpu.SemaphoreType.DMA
    attended, tile, logits_grad, w_big = pl.pallas_call(
        functools.partial(chain_kernel, ndp, nmp),
        out_shape=(
            jax.ShapeDtypeStruct((seq, full), BF),
            jax.ShapeDtypeStruct((tp, width), BF),
            jax.ShapeDtypeStruct((ntask, nsrc), F32),
            jax.ShapeDtypeStruct((tp, spn), BF),
        ),
        in_specs=[vmem, pl.BlockSpec(memory_space=pltpu.SMEM)] + [hbm] * 7,
        out_specs=(hbm, vmem, vmem, hbm),
        scratch_shapes=[
            pltpu.VMEM((seq, full), BF),
            pltpu.VMEM((tp, spn), BF),
            pltpu.VMEM((nsrc, rows, width), BF),
            pltpu.VMEM((full, width), BF),
            pltpu.VMEM((full, width), BF),
            pltpu.VMEM((seq, full), BF),
            pltpu.VMEM((seq, full), BF),
            pltpu.VMEM((seq, full), BF),
            pltpu.VMEM((seq, full), BF),
            pltpu.VMEM((nmp, tp, width), BF),
            pltpu.VMEM((ge, tp), F32),
            pltpu.VMEM((ndp, ge, tp), F32),
            pltpu.VMEM((n, 2, rows, width), BF),
            pltpu.VMEM((2, ptok, full), BF),
            pltpu.VMEM((2, ptok, full), BF),
            pltpu.VMEM((n, 2, rows, width), BF),
            pltpu.VMEM((nz, tp, width), BF),
            pltpu.VMEM((nz, tp, width), BF),
            pltpu.VMEM((nz, tp, width), BF),
            pltpu.VMEM((nz, tp, width), BF),
            pltpu.VMEM((ntask, nsrc), F32),
            pltpu.VMEM((n, ntask, nsrc), F32),
            dma((11,)),
            dma((nz,)), dma((nz,)), dma((nz,)), dma((nz,)),
            dma((ndp,)), dma((ndp,)),
            dma((n,)), dma((n,)), dma((n,)), dma((n,)),
            dma((nz,)), dma((nz,)), dma((nz,)), dma((nz,)),
            dma((n,)), dma((n,)),
        ],
        compiler_params=pltpu.CompilerParams(
            collective_id=0, has_side_effects=True, vmem_limit_bytes=60 * 2**20
        ),
        name="chain",
    )(
        task_logits, task_ids, source_prompts, key_weight, value_weight,
        queries.reshape(seq, full), keys.reshape(seq, full),
        values.reshape(seq, full), cotangent.reshape(seq, full),
    )
    steps = 2
    source_grad, attended, logits_grad = pl.pallas_call(
        source_kernel,
        grid=(steps,),
        out_shape=(
            jax.ShapeDtypeStruct((nsrc, rows, width), F32),
            jax.ShapeDtypeStruct((seq, full), BF),
            jax.ShapeDtypeStruct((ntask, nsrc), F32),
        ),
        in_specs=[
            pl.BlockSpec((tp, spn // steps), lambda i: (0, i)),
            pl.BlockSpec((tp, width), lambda i: (0, 0)),
            pl.BlockSpec((seq // steps, full), lambda i: (i, 0)),
            pl.BlockSpec((ntask, nsrc), lambda i: (0, 0)),
        ],
        out_specs=(
            pl.BlockSpec((nsrc // steps, rows, width), lambda i: (i, 0, 0)),
            pl.BlockSpec((seq // steps, full), lambda i: (i, 0)),
            pl.BlockSpec((ntask, nsrc), lambda i: (0, 0)),
        ),
        name="source_grad",
    )(w_big, tile, attended, logits_grad)
    return (attended.reshape(queries.shape), source_grad, logits_grad)


def solution(mesh):
    placed = (
        P(None, None, "mp"),
        P(),
        P("dp"),
        P(None, "mp"),
        P(None, "mp"),
        P(("dp", "mp"), None, None),
        P(("dp", "mp"), None, None),
        P(("dp", "mp"), None, None),
        P(("dp", "mp"), None, None),
    )
    return jax.shard_map(
        functools.partial(per_device, mesh.shape["dp"], mesh.shape["mp"]),
        mesh=mesh,
        in_specs=placed,
        out_specs=(P(("dp", "mp"), None, None), P(None, "dp", "mp"), P()),
        check_vma=False,
    )
```

profile of v0, /device:TPU:0, one launch (start us, length us, event | category | flops | bytes accessed | tf_op | source)
XLA Modules:
  0.0 105.5 jit_solution(6064105265034195135)
XLA Ops:
  0.6 100.9 %chain.1 = (bf16[128,4096]{1,0:T(8,128)(2,1)}, bf16[128,512]{1,0:T(8,128)(2,1)}, f32[8,128]{1,0:T(8,128)}, bf16[128,2048]{1,0:T(8,128)(2,1)}) custom-call(f32[8,128]{1,0:T(8,128)} %logits.1, s32[8]{0:T(128)} %ids_in.1, bf16[128,64,512]{2,1,0:T(8,128)(2,1)} %sp_hbm.1, bf16[4096,512]{1,0:T(8,128)(2,1)} %kw_hbm.1, bf16[4096,512]{1,0:T(8,128)(2,1)} %vw_hbm.1, ...), custom_call_target="tpu_custom_call" | custom-call | tf_op jit(solution)/shard_map/chain/pallas_call | solution.py:479
  101.6 4.0 %source_grad.1 = (f32[128,16,512]{2,1,0:T(8,128)}, bf16[128,4096]{1,0:T(8,128)(2,1)}, f32[8,128]{1,0:T(8,128)}) custom-call(bf16[128,2048]{1,0:T(8,128)(2,1)} %get-tuple-element.10.w_ref, bf16[128,512]{1,0:T(8,128)(2,1)} %get-tuple-element.11.tile_ref, bf16[128,4096]{1,0:T(8,128)(2,1)} %get-tuple-element.12.att_ref, f32[8,128]{1,0:T(8,128)} %get-tuple-element.13.lg_ref), custom_call_target="tpu_custom_call" | custom-call | tf_op jit(solution)/shard_map/source_grad/pallas_call | solution.py:529
where the time goes:
time: 106 us
  Pallas kernels  105 us (99%)
    pallas_call x1, Pallas kernels, per_device(): pl.pallas_call(functools.partial(chain_kernel, ndp, nmp), out_shape=(jax....  101 us
    pallas_call x1, Pallas kernels, per_device(): pl.pallas_call(source_kernel, grid=(steps,), out_shape=(jax.ShapeDtypeStr...  3.95 us

commit v1 on v0

--- a/solution.py
+++ b/solution.py
@@ -155,27 +155,36 @@
 
 
 def chain_kernel(
-    ndp, nmp,
+    ndp, nmp, nch,
     logits, ids_in, sp_hbm, kw_hbm, vw_hbm, q_hbm, k_hbm, v_hbm, c_hbm,
     att_hbm, tile_out, lg_out, w_hbm,
     att_out, w_out, p_v, kw_v, vw_v, q_v, k_v, v_v, c_v,
-    mixed, ids_own, ids_buf, sbuf, pair, gr, rbuf, ys, yr, zs, zr, wp, wbuf,
-    lsem, gs, gv, fs, fv, js, jv, bs, bv, cs, cv, us, uv, ts, tv, ws, wv,
+    mixed, ids_own, ids_buf, tab, sbuf, pair, gr, rbuf, acc, ubuf, urec, ys, yr, zs, zr, wp, wbuf,
+    lsem, gs, gv, fs, fv, js, jv, ts, tv, bs, bv, cs, cv, us, uv, hs, hv, es, ev, ws, wv,
 ):
     n = ndp * nmp
     nz = nmp // 2
+    ne = n // nz
     width = kw_v.shape[1]
+    cw = width // nch
     rows = p_v.shape[1]
     nsrc = p_v.shape[0]
     ntask = logits.shape[0]
     tp = ntask * rows
     spn = nsrc * rows
     seq = q_v.shape[0]
+    steps = nz * nch
     d = lax.axis_index("dp")
     m = lax.axis_index("mp")
     z = m // 2
-    y = m % 2
+    y = lax.rem(m, 2)
     me = d * nmp + m
+    own = y * ndp + d
+    up = 1 - 2 * (z // 2)
+    inner = lax.rem((z + 1) // 2, 2)
+    is_in = inner == 1
+    nxt = z + up
+    out_z = z - up * inner
     other = z * 2 + (1 - y)
 
     shift = rows.bit_length() - 1
@@ -194,6 +203,15 @@
             src_ref=src, dst_ref=dst, send_sem=ss, recv_sem=rs,
             device_id=(dd, mm_), device_id_type=pl.DeviceIdType.MESH,
         )
+
+    def place(i):
+        i = jnp.int32(i)
+        j = i - nch
+        mid = 1 - 2 * lax.rem(jnp.maximum(j, 0), 2)
+        off_in = jnp.where(i < nch, 0, jnp.where(i < 3 * nch, mid, 2))
+        h_in = jnp.where(i < nch, i, jnp.where(i < 3 * nch, jnp.maximum(j, 0) // 2, i - 3 * nch))
+        off = inner * off_in + (1 - inner) * (i // nch)
+        return z + up * off, inner * h_in + (1 - inner) * lax.rem(i, nch)
 
     barrier = pltpu.get_barrier_semaphore()
 
@@ -205,24 +223,29 @@
             device_id_type=pl.DeviceIdType.MESH,
         )
 
-    loads = [
-        pltpu.make_async_copy(
-            sp_hbm.at[:, pl.ds(pl.multiple_of(d * rows, rows), rows), :], p_v, lsem.at[0]
+    npl = 4
+    loads = []
+    for i in range(npl):
+        s_at = pl.ds(i * (nsrc // npl), nsrc // npl)
+        loads.append(
+            pltpu.make_async_copy(
+                sp_hbm.at[s_at, pl.ds(pl.multiple_of(d * rows, rows), rows), :],
+                p_v.at[s_at], lsem.at[9 + i],
+            )
         )
-    ]
+        loads[i].start()
     for i, (a, b) in enumerate(
         ((kw_hbm, kw_v), (vw_hbm, vw_v), (k_hbm, k_v), (q_hbm, q_v), (v_hbm, v_v), (c_hbm, c_v))
     ):
         loads.append(pltpu.make_async_copy(a, b, lsem.at[1 + i]))
-    loads[0].start()
 
     lg = logits[...]
     ex = jnp.exp(lg - jnp.max(lg, axis=1, keepdims=True))
     mix = ex / jnp.sum(ex, axis=1, keepdims=True)
-    up = (
+    upm = (
         outer(iota((tp, ntask), 0)) == iota((tp, ntask), 1)
     )
-    tall = mm(jnp.where(up, 1.0, 0.0), mix.astype(BF).astype(F32)).astype(BF)
+    tall = mm(jnp.where(upm, 1.0, 0.0), mix.astype(BF).astype(F32)).astype(BF)
     out = (
         outer(iota((nsrc, spn), 1)) == iota((nsrc, spn), 0)
     )
@@ -233,190 +256,349 @@
         ids_own[pl.ds(j, 1), :] = line
         ids_buf[d, pl.ds(j, 1), :] = line
 
-    loads[0].wait()
-    for c in loads[1:]:
+    for c in loads[:npl]:
+        c.wait()
+    for c in loads[npl:]:
         c.start()
-    w_save = pltpu.make_async_copy(w_out, w_hbm, lsem.at[9])
+    w_save = pltpu.make_async_copy(w_out, w_hbm, lsem.at[7])
     w_save.start()
-    mixed[m] = mm(w_out[...], p_v[...].reshape(spn, width)).astype(BF)
+    for h in range(nch):
+        mixed[m, h] = mm(w_out[...], p_v[:, :, pl.ds(h * cw, cw)].reshape(spn, cw)).astype(BF)
 
     pl.semaphore_wait(barrier, n - 1)
 
+    def g_copy(zz, h, dz):
+        k = zz * nch + h
+        slot = zz * 2 + y
+        return remote(mixed.at[slot, h], mixed.at[slot, h], gs.at[k], gv.at[k], d, dz * 2 + y)
+
+    def g2_copy(h):
+        k = nz * nch + h
+        slot = z * 2 + y
+        return remote(
+            mixed.at[slot, h], mixed.at[slot, h], gs.at[k], gv.at[z * nch + h], d, out_z * 2 + y
+        )
+
+    def f_copy(zz, h, yy):
+        k = zz * nch + h
+        slot = zz * 2 + yy
+        return remote(mixed.at[slot, h], mixed.at[slot, h], fs.at[k], fv.at[k], d, other)
+
+    for h in range(nch):
+        g_copy(z, h, nxt).start()
+
+        @pl.when(is_in)
+        def _():
+            g2_copy(h).start()
+
+        f_copy(z, h, y).start()
     idc = []
     for j in range(1, ndp):
         c = remote(ids_own, ids_buf.at[d], js.at[j], jv.at[j], lax.rem(d + j, ndp), m)
         c.start()
         idc.append(c)
-    gat = []
-    for j in range(1, nz):
-        c = remote(
-            mixed.at[m], mixed.at[m], gs.at[j], gv.at[j], d, lax.rem(z + j, nz) * 2 + y
-        )
-        c.start()
-        gat.append(c)
-    fwd = [remote(mixed.at[m], mixed.at[m], fs.at[0], fv.at[0], d, other)]
-    fwd[0].start()
+    loads[npl].wait()
+    loads[npl + 1].wait()
+
+    def part(slot, h):
+        block = mixed[slot, h]
+        at = pl.ds(pl.multiple_of(slot * width + h * cw, cw), cw)
+        return mm(block, kw_v[at, :]), mm(block, vw_v[at, :])
+
+    pk, pv = part(m, 0)
+    for h in range(1, nch):
+        a, b = part(m, h)
+        pk, pv = pk + a, pv + b
+    for i in range(nch, steps + nch):
+        if i < steps:
+            zz, h = place(i)
+            g_copy(zz, h, nxt).wait_recv()
+
+            @pl.when(is_in)
+            def _():
+                far = jnp.where(zz == out_z, nxt, out_z)
+                g_copy(zz, h, far).start()
+
+            f_copy(zz, h, y).start()
+            a, b = part(zz * 2 + y, h)
+            pk, pv = pk + a, pv + b
+        zz, h = place(i - nch)
+        f_copy(zz, h, 1 - y).wait_recv()
+        a, b = part(zz * 2 + (1 - y), h)
+        pk, pv = pk + a, pv + b
+    for h in range(nch):
+        at = slice(h * cw, (h + 1) * cw)
+        tab[z * nch + h, :, :cw] = pk[:, at].astype(BF)
+        tab[z * nch + h, :, cw:] = pv[:, at].astype(BF)
     for c in idc:
         c.wait()
-    loads[1].wait()
-    loads[2].wait()
-
-    def part(slot):
-        block = mixed[slot]
-        at = pl.ds(pl.multiple_of(slot * width, width), width)
-        return mm(block, kw_v[at, :]), mm(block, vw_v[at, :])
-
-    pk, pv = part(m)
-    for j in range(1, nz):
-        slot = lax.rem(z + nz - j, nz) * 2 + y
-        gat[j - 1].wait_recv()
-        c = remote(mixed.at[slot], mixed.at[slot], fs.at[j], fv.at[j], d, other)
-        c.start()
-        fwd.append(c)
-        a, b = part(slot)
-        pk, pv = pk + a, pv + b
-    for j in range(nz):
-        slot = lax.rem(z + nz - j, nz) * 2 + (1 - y)
-        fwd[j].wait_recv()
-        a, b = part(slot)
-        pk, pv = pk + a, pv + b
 
     ids_all = ids_buf[...].reshape(n, tp).astype(BF)
-    rep = (
-        outer(iota((n * rows, n), 0)) == iota((n * rows, n), 1)
-    )
-    ids_x = mm(jnp.where(rep, 1.0, 0.0).astype(BF), ids_all)
+    q_rows = 2 * ne * rows
+    q = outer(iota((q_rows, n), 0))
+    q_z = jnp.where(q < ne, z, out_z)
+    q_in = q & (ne - 1)
+    q_dev = lax.rem(q_in, jnp.int32(ndp)) * nmp + q_z * 2 + q_in // jnp.int32(ndp)
+    ids_x = mm(jnp.where(q_dev == iota((q_rows, n), 1), 1.0, 0.0).astype(BF), ids_all)
     sel = jnp.where(
-        (ids_x == outer(iota((n * rows, tp), 1)).astype(F32)) & same_row((n * rows, tp)), 1.0, 0.0
+        (ids_x == outer(iota((q_rows, tp), 1)).astype(F32)) & same_row((q_rows, tp)), 1.0, 0.0
     ).astype(BF)
-    sbuf[:, 0] = mm(sel, pk.astype(BF)).astype(BF).reshape(n, rows, width)
-    sbuf[:, 1] = mm(sel, pv.astype(BF)).astype(BF).reshape(n, rows, width)
-
-    my_rows = pl.ds(pl.multiple_of(d * rows, rows), rows)
-    my_cols = pl.ds(pl.multiple_of(m * width, width), width)
-
-    def b_copy(k):
-        dd, gg = lax.rem(k, ndp), k // ndp
-        td, tm = lax.rem(d + ndp - dd, ndp), lax.rem(m + nmp - gg, nmp)
+    sel_own = sel[: ne * rows]
+
+    def row_at(dd):
+        return pl.ds(pl.multiple_of(dd * rows, rows), rows)
+
+    def col_at(zz, yy, h):
+        return pl.ds(pl.multiple_of((zz * 2 + yy) * width + h * cw, cw), cw)
+
+    def t_copy(zz, h):
+        k = zz * nch + h
+        return remote(tab.at[k], tab.at[k], ts.at[k], tv.at[k], d, nxt * 2 + y)
+
+    def b_copy(zz, h, e, to_out):
+        k = zz * nch + h
+        g = e + to_out * ne
         return remote(
-            sbuf.at[td * nmp + tm], pair.at[:, my_rows, my_cols], bs.at[k], bv.at[k], td, tm
+            sbuf.at[k, g], pair.at[:, row_at(d), col_at(zz, y, h)],
+            bs.at[k * 2 * ne + g], bv.at[k * ne + own],
+            lax.rem(e, ndp), (out_z if to_out else z) * 2 + e // ndp,
         )
 
-    own_b = pltpu.make_async_copy(sbuf.at[me], pair.at[:, my_rows, my_cols], lsem.at[7])
-    own_b.start()
-
-    def turn(t):
-        return lax.rem(t + nmp // 2 - 1 + t // (nmp // 2 + 1), nmp)
-
-    @pl.loop(1, nmp)
-    def _(t):
-        @pl.loop(0, ndp)
-        def _(dd):
-            b_copy(turn(t) * ndp + dd).start()
-
-    @pl.loop(1, ndp)
-    def _(dd):
-        b_copy(dd).start()
-
-    for c in loads[3:]:
+    def b_wait(zz, h, e):
+        k = zz * nch + h
+        remote(
+            sbuf.at[k, e], pair.at[:, row_at(lax.rem(e, ndp)), col_at(zz, e // ndp, h)],
+            bs.at[k * 2 * ne + e], bv.at[k * ne + e], d, other,
+        ).wait_recv()
+
+    def relay(i):
+        zz, h = place(i)
+        k = zz * nch + h
+
+        @pl.when(zz != z)
+        def _():
+            t_copy(zz, h).wait_recv()
+
+        @pl.when((zz == z) | (zz == out_z))
+        def _():
+            t_copy(zz, h).start()
+
+        got = mm(sel, tab[k]).astype(BF)
+        sbuf[k, :, 0] = got[:, :cw].reshape(2 * ne, rows, cw)
+        sbuf[k, :, 1] = got[:, cw:].reshape(2 * ne, rows, cw)
+
+        @pl.when(is_in & (zz != out_z))
+        def _():
+            @pl.loop(0, ne)
+            def _(r):
+                b_copy(zz, h, lax.rem(own + r, ne), 1).start()
+
+        @pl.loop(1, ne)
+        def _(r):
+            b_copy(zz, h, lax.rem(own + r, ne), 0).start()
+
+        pair[:, row_at(d), col_at(zz, y, h)] = sbuf[k, own]
+
+    for i in range(nch):
+        relay(i)
+
+    for c in loads[npl + 2:]:
         c.wait()
-    own_b.wait()
-
-    def c_copy(k):
-        dd, gg = lax.rem(k, ndp), k // ndp
-        td, tm = lax.rem(d + dd, ndp), lax.rem(m + gg, nmp)
+
+    def c_copy(zz, h, e):
+        k = zz * nch + h
         return remote(
-            gr.at[
-                :,
-                pl.ds(pl.multiple_of(td * rows, rows), rows),
-                pl.ds(pl.multiple_of(tm * width, width), width),
-            ],
-            rbuf.at[me], cs.at[k], cv.at[k], td, tm,
+            gr.at[:, row_at(lax.rem(e, ndp)), col_at(zz, e // ndp, h)], rbuf.at[k, own],
+            cs.at[k * ne + e], cv.at[k * ne + own], lax.rem(e, ndp), z * 2 + e // ndp,
         )
+
+    def c_wait(zz, h, e):
+        k = zz * nch + h
+        remote(
+            gr.at[:, row_at(lax.rem(e, ndp)), col_at(zz, e // ndp, h)], rbuf.at[k, e],
+            cs.at[k * ne + e], cv.at[k * ne + e], d, other,
+        ).wait_recv()
 
     scale = DH ** (-0.5)
     to_exp2 = scale * 1.4426950408889634
     ptok = pair.shape[1]
     seen = iota((seq, seq), 0) <= iota((seq, seq), 1)
 
-    def group(g, wait_from):
-        @pl.loop(wait_from, ndp)
-        def _(dd):
-            b_copy(g * ndp + dd).wait_recv()
-
-        base = lax.rem(m + g, nmp) * width
+    def group(i):
+        zz, h = place(i)
+
+        @pl.when(is_in | (zz == z))
+        def _():
+            @pl.loop(1, ne)
+            def _(r):
+                b_wait(zz, h, lax.rem(own + r, ne))
+
+        @pl.when(jnp.logical_not(is_in | (zz == z)))
+        def _():
+            @pl.loop(0, ne)
+            def _(r):
+                b_wait(zz, h, r)
+
         ats, st, gt, va = [], [], [], []
-        for h in range(width // DH):
-            at = pl.ds(pl.multiple_of(base + h * DH, DH), DH)
-            ats.append(at)
-            ka = jnp.concatenate([pair[0, :, at], k_v[:, at]], axis=0)
-            va.append(jnp.concatenate([pair[1, :, at], v_v[:, at]], axis=0))
-            st.append(mm(ka, q_v[:, at], 1, 1))
-            gt.append(mm(va[h], c_v[:, at], 1, 1))
-        for h in range(width // DH):
-            at = ats[h]
-            s = st[h] * to_exp2
+        for yy in range(2):
+            for hh in range(cw // DH):
+                base = (zz * 2 + yy) * width + h * cw + hh * DH
+                at = pl.ds(pl.multiple_of(base, DH), DH)
+                ats.append(at)
+                ka = jnp.concatenate([pair[0, :, at], k_v[:, at]], axis=0)
+                va.append(jnp.concatenate([pair[1, :, at], v_v[:, at]], axis=0))
+                st.append(mm(ka, q_v[:, at], 1, 1))
+                gt.append(mm(va[-1], c_v[:, at], 1, 1))
+        for j, at in enumerate(ats):
+            s = st[j] * to_exp2
             s = jnp.concatenate([s[:ptok], jnp.where(seen, s[ptok:], mask_fill)], axis=0)
             e = jnp.exp2(s - jnp.max(s, axis=0, keepdims=True))
             a = e * (1.0 / jnp.sum(e, axis=0, keepdims=True))
             ab = a.astype(BF)
-            inner = jnp.sum(a * gt[h], axis=0, keepdims=True)
-            gs1 = (a[:ptok] * (gt[h][:ptok] - inner)).astype(BF)
+            inner_sum = jnp.sum(a * gt[j], axis=0, keepdims=True)
+            gs1 = (a[:ptok] * (gt[j][:ptok] - inner_sum)).astype(BF)
             gr[0, :, at] = (mm(gs1, q_v[:, at]) * scale).astype(BF)
             gr[1, :, at] = mm(ab[:ptok], c_v[:, at]).astype(BF)
-            att_out[:, at] = mm(ab, va[h], 0, 0).astype(BF)
-
-    group(0, 1)
-    own_c = pltpu.make_async_copy(gr.at[:, my_rows, my_cols], rbuf.at[me], lsem.at[8])
-    own_c.start()
-
-    @pl.loop(1, ndp)
-    def _(dd):
-        c_copy(dd).start()
-
-    @pl.loop(1, nmp)
-    def _(t):
-        g = turn(t)
-        group(g, 0)
-
-        @pl.loop(0, ndp)
-        def _(dd):
-            c_copy(g * ndp + dd).start()
-
-    own_c.wait()
-    att_save = pltpu.make_async_copy(att_out, att_hbm, lsem.at[10])
+            att_out[:, at] = mm(ab, va[j], 0, 0).astype(BF)
+
+        @pl.loop(1, ne)
+        def _(r):
+            c_copy(zz, h, lax.rem(own + r, ne)).start()
+
+        rbuf[zz * nch + h, own] = gr[:, row_at(d), col_at(zz, y, h)]
+
+    def u_copy(zz, h, dz, slot):
+        k = zz * nch + h
+        return remote(
+            ubuf.at[k], urec.at[slot * nch + h], us.at[k], uv.at[slot * nch + h], d, dz * 2 + y
+        )
+
+    def total(i):
+        zz, h = place(i)
+        k = zz * nch + h
+
+        @pl.loop(1, ne)
+        def _(r):
+            c_wait(zz, h, lax.rem(own + r, ne))
+
+        acc[k, :, :cw] = mm(sel_own, rbuf[k, :, 0].reshape(ne * rows, cw), 0, 0)
+        acc[k, :, cw:] = mm(sel_own, rbuf[k, :, 1].reshape(ne * rows, cw), 0, 0)
+
+        @pl.when(is_in & (zz == out_z))
+        def _():
+            ubuf[k] = acc[k].astype(BF)
+            u_copy(zz, h, out_z, z).start()
+
+        @pl.when(jnp.logical_not(is_in | (zz == z)))
+        def _():
+            ubuf[k] = acc[k].astype(BF)
+            u_copy(zz, h, nxt, zz).start()
+
+    @pl.loop(0, steps)
+    def _(i):
+        @pl.when(is_in & (i < steps - nch))
+        def _():
+            relay(i + nch)
+
+        group(i)
+
+        @pl.when(i >= nch)
+        def _():
+            total(i - nch)
+
+    att_save = pltpu.make_async_copy(att_out, att_hbm, lsem.at[8])
     att_save.start()
 
-    @pl.loop(1, n)
-    def _(k):
-        c_copy(k).wait_recv()
-
-    tk = mm(sel, rbuf[:, 0].reshape(n * rows, width), 0, 0).astype(BF)
-    tv_ = mm(sel, rbuf[:, 1].reshape(n * rows, width), 0, 0).astype(BF)
-
-    def term(slot):
-        at = pl.ds(pl.multiple_of(slot * width, width), width)
+    @pl.loop(steps - nch, steps)
+    def _(i):
+        total(i)
+
+    far = ((1, z + 2 * up), (2, z))
+
+    def u_far(off, slot, h):
+        return u_copy(z + up * off, h, z + up * off, slot)
+
+    @pl.when(is_in)
+    def _():
+        for off, slot in far:
+            for h in range(nch):
+                zz = z + up * off
+                k = zz * nch + h
+                u_copy(zz, h, zz, zz).wait_recv()
+                ubuf[k] = (acc[k] + urec[k].astype(F32)).astype(BF)
+                u_far(off, slot, h).start()
+
+    s1 = z + up * (1 - inner)
+    s2 = z + up * (2 - 3 * inner)
+    tks, tvs = [], []
+    for h in range(nch):
+        u_copy(z, h, nxt, s1).wait_recv()
+        u_copy(z, h, nxt, s2).wait_recv()
+        t = acc[z * nch + h] + urec[s1 * nch + h].astype(F32) + urec[s2 * nch + h].astype(F32)
+        t = t.astype(BF)
+        tks.append(t[:, :cw])
+        tvs.append(t[:, cw:])
+    tk = jnp.concatenate(tks, axis=1)
+    tv_ = jnp.concatenate(tvs, axis=1)
+
+    def term(slot, h):
+        at = pl.ds(pl.multiple_of(slot * width + h * cw, cw), cw)
         return mm(tk, kw_v[at, :], 1, 1) + mm(tv_, vw_v[at, :], 1, 1)
 
-    yc, zc = [None] * nz, [None] * nz
-    order = list(range(1, nz)) + [0]
-    for j in order:
-        ys[j] = term(lax.rem(z + j, nz) * 2 + (1 - y)).astype(BF)
-        yc[j] = remote(ys.at[j], yr.at[j], us.at[j], uv.at[j], d, other)
-        yc[j].start()
-    for j in order:
-        to = lax.rem(z + j, nz) * 2 + y
-        mine = term(to)
-        yc[j].wait_recv()
-        mine = mine + yr[j].astype(F32)
-        if j:
-            zs[j] = mine.astype(BF)
-            zc[j] = remote(zs.at[j], zr.at[j], ts.at[j], tv.at[j], d, to)
-            zc[j].start()
-    for j in range(1, nz):
-        zc[j].wait_recv()
-        mine = mine + zr[j].astype(F32)
-    tile = mine.astype(BF)
+    def target(j):
+        return z + up * ((nz - 1 - j) * (1 - inner) + inner * (2, 1, -1, 0)[j])
+
+    def y_copy(j, h):
+        k = j * nch + h
+        return remote(ys.at[k], yr.at[k], hs.at[k], hv.at[k], d, other)
+
+    def z_copy(zz, h, dz, slot):
+        k = zz * nch + h
+        return remote(
+            zs.at[k], zr.at[slot * nch + h], es.at[k], ev.at[slot * nch + h], d, dz * 2 + y
+        )
+
+    for j in range(nz):
+        for h in range(nch):
+            ys[j * nch + h] = term(target(j) * 2 + (1 - y), h).astype(BF)
+            y_copy(j, h).start()
+
+    def route(j):
+        zz = target(j)
+        if j == 0:
+            return jnp.where(is_in, zz, nxt), jnp.where(is_in, z, zz)
+        if j == 1:
+            return jnp.where(is_in, zz, nxt), jnp.where(is_in, z + 2 * up, zz)
+        return jnp.where(is_in, out_z, nxt), jnp.where(is_in, z, zz)
+
+    tile = []
+    for j in range(nz):
+        zz = target(j)
+        for h in range(nch):
+            k = zz * nch + h
+            mine = term(zz * 2 + y, h)
+            y_copy(j, h).wait_recv()
+            mine = mine + yr[j * nch + h].astype(F32)
+            if j == nz - 1:
+                z_copy(z, h, nxt, s1).wait_recv()
+                z_copy(z, h, nxt, s2).wait_recv()
+                mine = mine + zr[s1 * nch + h].astype(F32) + zr[s2 * nch + h].astype(F32)
+                tile.append(mine.astype(BF))
+                continue
+            if j < 2:
+                acc[k, :, :cw] = mine
+
+                @pl.when(is_in)
+                def _():
+                    z_copy(zz, h, zz, zz).wait_recv()
+                    acc[k, :, :cw] = acc[k, :, :cw] + zr[k].astype(F32)
+
+                zs[k] = acc[k, :, :cw].astype(BF)
+            else:
+                zs[k] = mine.astype(BF)
+            dz, slot = route(j)
+            z_copy(zz, h, dz, slot).start()
+    tile = jnp.concatenate(tile, axis=1)
     tile_out[...] = tile
 
     prod = mm(p_v[...].reshape(spn, width), tile, 1, 1)
@@ -438,13 +620,57 @@
 
     w_save.wait()
     att_save.wait()
-    for c in gat + fwd + yc + zc[1:]:
-        c.wait_send()
-
-    @pl.loop(1, n)
-    def _(k):
-        b_copy(k).wait_send()
-        c_copy(k).wait_send()
+
+    for h in range(nch):
+        g_copy(z, h, nxt).wait_send()
+        f_copy(z, h, y).wait_send()
+        t_copy(z, h).wait_send()
+
+    @pl.loop(nch, steps)
+    def _(i):
+        zz, h = place(i)
+        f_copy(zz, h, y).wait_send()
+
+        @pl.when(is_in)
+        def _():
+            g_copy(zz, h, nxt).wait_send()
+
+        @pl.when(is_in & (zz == out_z))
+        def _():
+            t_copy(zz, h).wait_send()
+
+        u_copy(zz, h, nxt, s1).wait_send()
+
+    @pl.when(is_in)
+    def _():
+        for h in range(nch):
+            g2_copy(h).wait_send()
+
+    for j in range(nz):
+        for h in range(nch):
+            y_copy(j, h).wait_send()
+            if j < nz - 1:
+                z_copy(target(j), h, nxt, s1).wait_send()
+
+    @pl.loop(0, steps)
+    def _(i):
+        zz, h = place(i)
+
+        @pl.loop(1, ne)
+        def _(r):
+            c_copy(zz, h, lax.rem(own + r, ne)).wait_send()
+
+        @pl.when(is_in | (zz == z))
+        def _():
+            @pl.loop(1, ne)
+            def _(r):
+                b_copy(zz, h, lax.rem(own + r, ne), 0).wait_send()
+
+        @pl.when(is_in & (zz != out_z))
+        def _():
+            @pl.loop(0, ne)
+            def _(r):
+                b_copy(zz, h, r, 1).wait_send()
 
     @pl.loop(1, n)
     def _(k):
@@ -468,16 +694,18 @@
     ntask = task_logits.shape[0]
     ge = task_ids.shape[0]
     rows = ptok // ndp
-    if width % DH or nmp % 4 or ge != nmp or ptok % ndp or rows % 16 or rows & (rows - 1) or ntask * rows != 128:
+    nch = 2
+    if width % (nch * DH) or nmp != 8 or ndp & (ndp - 1) or ge != nmp or ptok % ndp or rows % 16 or rows & (rows - 1) or ntask * rows != 128:
         return on_device(*args)
     n, nz = ndp * nmp, nmp // 2
+    ne, st, cw = n // nz, nz * nch, width // nch
     tp, spn = ntask * rows, nsrc * rows
     seq, full = queries.shape[1:]
     vmem = pl.BlockSpec(memory_space=pltpu.VMEM)
     hbm = pl.BlockSpec(memory_space=pl.ANY)
     dma = pltpu.SemaphoreType.DMA
     attended, tile, logits_grad, w_big = pl.pallas_call(
-        functools.partial(chain_kernel, ndp, nmp),
+        functools.partial(chain_kernel, ndp, nmp, nch),
         out_shape=(
             jax.ShapeDtypeStruct((seq, full), BF),
             jax.ShapeDtypeStruct((tp, width), BF),
@@ -496,24 +724,29 @@
             pltpu.VMEM((seq, full), BF),
             pltpu.VMEM((seq, full), BF),
             pltpu.VMEM((seq, full), BF),
-            pltpu.VMEM((nmp, tp, width), BF),
+            pltpu.VMEM((nmp, nch, tp, cw), BF),
             pltpu.VMEM((ge, tp), F32),
             pltpu.VMEM((ndp, ge, tp), F32),
-            pltpu.VMEM((n, 2, rows, width), BF),
+            pltpu.VMEM((st, tp, 2 * cw), BF),
+            pltpu.VMEM((st, 2 * ne, 2, rows, cw), BF),
             pltpu.VMEM((2, ptok, full), BF),
             pltpu.VMEM((2, ptok, full), BF),
-            pltpu.VMEM((n, 2, rows, width), BF),
-            pltpu.VMEM((nz, tp, width), BF),
-            pltpu.VMEM((nz, tp, width), BF),
-            pltpu.VMEM((nz, tp, width), BF),
-            pltpu.VMEM((nz, tp, width), BF),
+            pltpu.VMEM((st, ne, 2, rows, cw), BF),
+            pltpu.VMEM((st, tp, 2 * cw), F32),
+            pltpu.VMEM((st, tp, 2 * cw), BF),
+            pltpu.VMEM((st, tp, 2 * cw), BF),
+            pltpu.VMEM((st, tp, cw), BF),
+            pltpu.VMEM((st, tp, cw), BF),
+            pltpu.VMEM((st, tp, cw), BF),
+            pltpu.VMEM((st, tp, cw), BF),
             pltpu.VMEM((ntask, nsrc), F32),
             pltpu.VMEM((n, ntask, nsrc), F32),
-            dma((11,)),
-            dma((nz,)), dma((nz,)), dma((nz,)), dma((nz,)),
+            dma((13,)),
+            dma((st + nch,)), dma((st,)), dma((st,)), dma((st,)),
             dma((ndp,)), dma((ndp,)),
-            dma((n,)), dma((n,)), dma((n,)), dma((n,)),
-            dma((nz,)), dma((nz,)), dma((nz,)), dma((nz,)),
+            dma((st,)), dma((st,)),
+            dma((st * 2 * ne,)), dma((st * ne,)), dma((st * ne,)), dma((st * ne,)),
+            dma((st,)), dma((st,)), dma((st,)), dma((st,)), dma((st,)), dma((st,)),
             dma((n,)), dma((n,)),
         ],
         compiler_params=pltpu.CompilerParams(

time: 106 us -> 99.2 us (0.936)
  Pallas kernels: 105 us -> 98.3 us
    pallas_call x1, Pallas kernels: 101 us -> 94.4 us  [per_device(): pl.pallas_call(functools.partial(chain_kernel, ndp, nmp, nch), out_shape=...]
where the time goes in v1:
time: 99.2 us; the launch traced here: 99 us
  Pallas kernels  98.3 us (99%)
    pallas_call x1, Pallas kernels, per_device(): pl.pallas_call(functools.partial(chain_kernel, ndp, nmp, nch), out_shape=...  94.4 us
    pallas_call x1, Pallas kernels, per_device(): pl.pallas_call(source_kernel, grid=(steps,), out_shape=(jax.ShapeDtypeStr...  3.95 us

profile of v1, /device:TPU:0, one launch (start us, length us, event | category | flops | bytes accessed | tf_op | source)
XLA Modules:
  0.0 99.0 jit_solution(14623515047539079925)
XLA Ops:
  0.6 94.4 %chain.1 = (bf16[128,4096]{1,0:T(8,128)(2,1)}, bf16[128,512]{1,0:T(8,128)(2,1)}, f32[8,128]{1,0:T(8,128)}, bf16[128,2048]{1,0:T(8,128)(2,1)}) custom-call(f32[8,128]{1,0:T(8,128)} %logits.1, s32[8]{0:T(128)} %ids_in.1, bf16[128,64,512]{2,1,0:T(8,128)(2,1)} %sp_hbm.1, bf16[4096,512]{1,0:T(8,128)(2,1)} %kw_hbm.1, bf16[4096,512]{1,0:T(8,128)(2,1)} %vw_hbm.1, ...), custom_call_target="tpu_custom_call" | custom-call | tf_op jit(solution)/shard_map/chain/pallas_call | solution.py:707
  95.0 4.0 %source_grad.1 = (f32[128,16,512]{2,1,0:T(8,128)}, bf16[128,4096]{1,0:T(8,128)(2,1)}, f32[8,128]{1,0:T(8,128)}) custom-call(bf16[128,2048]{1,0:T(8,128)(2,1)} %get-tuple-element.10.w_ref, bf16[128,512]{1,0:T(8,128)(2,1)} %get-tuple-element.11.tile_ref, bf16[128,4096]{1,0:T(8,128)(2,1)} %get-tuple-element.12.att_ref, f32[8,128]{1,0:T(8,128)} %get-tuple-element.13.lg_ref), custom_call_target="tpu_custom_call" | custom-call | tf_op jit(solution)/shard_map/source_grad/pallas_call | solution.py:762

commit v2 on v1

--- a/solution.py
+++ b/solution.py
@@ -156,10 +156,10 @@
 
 def chain_kernel(
     ndp, nmp, nch,
-    logits, ids_in, sp_hbm, kw_hbm, vw_hbm, q_hbm, k_hbm, v_hbm, c_hbm,
-    att_hbm, tile_out, lg_out, w_hbm,
-    att_out, w_out, p_v, kw_v, vw_v, q_v, k_v, v_v, c_v,
-    mixed, ids_own, ids_buf, tab, sbuf, pair, gr, rbuf, acc, ubuf, urec, ys, yr, zs, zr, wp, wbuf,
+    lg_hbm, ids_hbm, sp_hbm, kw_hbm, vw_hbm, q_hbm, k_hbm, v_hbm, c_hbm,
+    att_hbm, tile_hbm, lg_out, w_hbm,
+    logits, ids_in, tile_v, att_out, w_out, p_v, kw_v, vw_v, q_v, k_v, v_v, c_v,
+    mixed, ids_own, ids_buf, tab, sbuf, pair, gr, rbuf, acc, ubuf, urec, ys, yr, zs, zr, zt, wp, wbuf,
     lsem, gs, gv, fs, fv, js, jv, ts, tv, bs, bv, cs, cv, us, uv, hs, hv, es, ev, ws, wv,
 ):
     n = ndp * nmp
@@ -204,14 +204,42 @@
             device_id=(dd, mm_), device_id_type=pl.DeviceIdType.MESH,
         )
 
+    def drain(ref, sem):
+        pltpu.make_async_copy(ref, ref, sem).wait()
+
     def place(i):
         i = jnp.int32(i)
-        j = i - nch
-        mid = 1 - 2 * lax.rem(jnp.maximum(j, 0), 2)
-        off_in = jnp.where(i < nch, 0, jnp.where(i < 3 * nch, mid, 2))
-        h_in = jnp.where(i < nch, i, jnp.where(i < 3 * nch, jnp.maximum(j, 0) // 2, i - 3 * nch))
-        off = inner * off_in + (1 - inner) * (i // nch)
-        return z + up * off, inner * h_in + (1 - inner) * lax.rem(i, nch)
+        k = i // nch
+        off_in = jnp.where(k == 2, -1, jnp.where(k == 3, 2, k))
+        return z + up * (inner * off_in + (1 - inner) * k), lax.rem(i, nch)
+
+    small = [
+        pltpu.make_async_copy(lg_hbm, logits, lsem.at[9]),
+        pltpu.make_async_copy(ids_hbm, ids_in, lsem.at[10]),
+    ]
+    for c in small:
+        c.start()
+    npl = 4
+    loads = []
+    for i in range(npl):
+        s_at = pl.ds(i * (nsrc // npl), nsrc // npl)
+        loads.append(
+            pltpu.make_async_copy(
+                sp_hbm.at[s_at, pl.ds(pl.multiple_of(d * rows, rows), rows), :],
+                p_v.at[s_at], lsem.at[0],
+            )
+        )
+        loads[i].start()
+    for i, (a, b) in enumerate(
+        ((kw_hbm, kw_v), (vw_hbm, vw_v), (k_hbm, k_v), (q_hbm, q_v), (v_hbm, v_v), (c_hbm, c_v))
+    ):
+        loads.append(pltpu.make_async_copy(a, b, lsem.at[1 + i]))
+
+    def turn(i):
+        i = jnp.int32(i)
+        zz, h = place(i)
+        late = z + up * lax.rem(i // nch + 1, nz)
+        return jnp.where(is_in, zz, late), h
 
     barrier = pltpu.get_barrier_semaphore()
 
@@ -223,22 +251,8 @@
             device_id_type=pl.DeviceIdType.MESH,
         )
 
-    npl = 4
-    loads = []
-    for i in range(npl):
-        s_at = pl.ds(i * (nsrc // npl), nsrc // npl)
-        loads.append(
-            pltpu.make_async_copy(
-                sp_hbm.at[s_at, pl.ds(pl.multiple_of(d * rows, rows), rows), :],
-                p_v.at[s_at], lsem.at[9 + i],
-            )
-        )
-        loads[i].start()
-    for i, (a, b) in enumerate(
-        ((kw_hbm, kw_v), (vw_hbm, vw_v), (k_hbm, k_v), (q_hbm, q_v), (v_hbm, v_v), (c_hbm, c_v))
-    ):
-        loads.append(pltpu.make_async_copy(a, b, lsem.at[1 + i]))
-
+    for c in small:
+        c.wait()
     lg = logits[...]
     ex = jnp.exp(lg - jnp.max(lg, axis=1, keepdims=True))
     mix = ex / jnp.sum(ex, axis=1, keepdims=True)
@@ -256,8 +270,7 @@
         ids_own[pl.ds(j, 1), :] = line
         ids_buf[d, pl.ds(j, 1), :] = line
 
-    for c in loads[:npl]:
-        c.wait()
+    pltpu.make_async_copy(p_v, p_v, lsem.at[0]).wait()
     for c in loads[npl:]:
         c.start()
     w_save = pltpu.make_async_copy(w_out, w_hbm, lsem.at[7])
@@ -268,35 +281,36 @@
     pl.semaphore_wait(barrier, n - 1)
 
     def g_copy(zz, h, dz):
-        k = zz * nch + h
         slot = zz * 2 + y
-        return remote(mixed.at[slot, h], mixed.at[slot, h], gs.at[k], gv.at[k], d, dz * 2 + y)
-
-    def g2_copy(h):
-        k = nz * nch + h
-        slot = z * 2 + y
         return remote(
-            mixed.at[slot, h], mixed.at[slot, h], gs.at[k], gv.at[z * nch + h], d, out_z * 2 + y
+            mixed.at[slot, h], mixed.at[slot, h], gs.at[0], gv.at[zz * nch + h], d, dz * 2 + y
         )
 
     def f_copy(zz, h, yy):
-        k = zz * nch + h
         slot = zz * 2 + yy
-        return remote(mixed.at[slot, h], mixed.at[slot, h], fs.at[k], fv.at[k], d, other)
+        return remote(
+            mixed.at[slot, h], mixed.at[slot, h], fs.at[0], fv.at[zz * nch + h], d, other
+        )
 
     for h in range(nch):
-        g_copy(z, h, nxt).start()
+        f_copy(z, h, y).start()
 
         @pl.when(is_in)
         def _():
-            g2_copy(h).start()
-
-        f_copy(z, h, y).start()
-    idc = []
+            g_copy(z, h, out_z).start()
+            g_copy(z, h, nxt).start()
+
+        @pl.when(jnp.logical_not(is_in))
+        def _():
+            g_copy(z, h, nxt).start()
+
+    @pl.when(jnp.logical_not(is_in))
+    def _():
+        for h in range(nch):
+            g_copy(z, h, z + 3 * up).start()
+
     for j in range(1, ndp):
-        c = remote(ids_own, ids_buf.at[d], js.at[j], jv.at[j], lax.rem(d + j, ndp), m)
-        c.start()
-        idc.append(c)
+        remote(ids_own, ids_buf.at[d], js.at[0], jv.at[0], lax.rem(d + j, ndp), m).start()
     loads[npl].wait()
     loads[npl + 1].wait()
 
@@ -309,29 +323,50 @@
     for h in range(1, nch):
         a, b = part(m, h)
         pk, pv = pk + a, pv + b
-    for i in range(nch, steps + nch):
-        if i < steps:
-            zz, h = place(i)
-            g_copy(zz, h, nxt).wait_recv()
-
+    arrive = [(0, 0, h, h) for h in range(nch)]
+    arrive += [(1, 1 - 2 * (i % 2), i, i // 2) for i in range(nch)]
+    for i in range(2 * nch):
+        k = nch + i
+        side = (1 - 2 * (k % 2), k // 2) if k < 2 * nch else (2, k - 2 * nch)
+        arrive.append((2 + i % 2, side[0], i // 2, side[1]))
+
+    def arrival(i):
+        off_o, off_i, h_o, h_i = arrive[i]
+        return z + up * (off_o + inner * (off_i - off_o)), h_o + inner * (h_i - h_o)
+
+    def from_z(i, pk, pv):
+        zz, h = arrival(i)
+        g_copy(zz, h, nxt).wait_recv()
+        if arrive[i][1] != 2:
             @pl.when(is_in)
             def _():
-                far = jnp.where(zz == out_z, nxt, out_z)
-                g_copy(zz, h, far).start()
-
-            f_copy(zz, h, y).start()
-            a, b = part(zz * 2 + y, h)
-            pk, pv = pk + a, pv + b
-        zz, h = place(i - nch)
+                g_copy(zz, h, out_z if arrive[i][1] == 1 else nxt).start()
+
+        f_copy(zz, h, y).start()
+        a, b = part(zz * 2 + y, h)
+        return pk + a, pv + b
+
+    def from_y(i, pk, pv):
+        zz, h = arrival(i)
         f_copy(zz, h, 1 - y).wait_recv()
         a, b = part(zz * 2 + (1 - y), h)
-        pk, pv = pk + a, pv + b
+        return pk + a, pv + b
+
+    lag = 2 * nch
+    for i in range(nch, steps + lag):
+        if i < steps:
+            pk, pv = from_z(i, pk, pv)
+        if i >= lag:
+            pk, pv = from_y(i - lag, pk, pv)
     for h in range(nch):
         at = slice(h * cw, (h + 1) * cw)
         tab[z * nch + h, :, :cw] = pk[:, at].astype(BF)
         tab[z * nch + h, :, cw:] = pv[:, at].astype(BF)
-    for c in idc:
-        c.wait()
+        remote(
+            tab.at[z * nch + h], tab.at[z * nch + h], ts.at[0], tv.at[z * nch + h],
+            d, nxt * 2 + y,
+        ).start()
+    drain(ids_buf.at[pl.ds(0, ndp - 1)], jv.at[0])
 
     ids_all = ids_buf[...].reshape(n, tp).astype(BF)
     q_rows = 2 * ne * rows
@@ -351,25 +386,18 @@
     def col_at(zz, yy, h):
         return pl.ds(pl.multiple_of((zz * 2 + yy) * width + h * cw, cw), cw)
 
-    def t_copy(zz, h):
+    def t_copy(zz, h, dz):
         k = zz * nch + h
-        return remote(tab.at[k], tab.at[k], ts.at[k], tv.at[k], d, nxt * 2 + y)
+        return remote(tab.at[k], tab.at[k], ts.at[0], tv.at[k], d, dz * 2 + y)
 
     def b_copy(zz, h, e, to_out):
         k = zz * nch + h
         g = e + to_out * ne
         return remote(
-            sbuf.at[k, g], pair.at[:, row_at(d), col_at(zz, y, h)],
-            bs.at[k * 2 * ne + g], bv.at[k * ne + own],
+            sbuf.at[k * 2 * ne + g], pair.at[:, row_at(d), col_at(zz, y, h)],
+            bs.at[0], bv.at[k],
             lax.rem(e, ndp), (out_z if to_out else z) * 2 + e // ndp,
         )
-
-    def b_wait(zz, h, e):
-        k = zz * nch + h
-        remote(
-            sbuf.at[k, e], pair.at[:, row_at(lax.rem(e, ndp)), col_at(zz, e // ndp, h)],
-            bs.at[k * 2 * ne + e], bv.at[k * ne + e], d, other,
-        ).wait_recv()
 
     def relay(i):
         zz, h = place(i)
@@ -377,30 +405,40 @@
 
         @pl.when(zz != z)
         def _():
-            t_copy(zz, h).wait_recv()
-
-        @pl.when((zz == z) | (zz == out_z))
-        def _():
-            t_copy(zz, h).start()
+            t_copy(zz, h, nxt).wait_recv()
+
+        @pl.when(is_in & (zz == out_z))
+        def _():
+            t_copy(zz, h, nxt).start()
 
         got = mm(sel, tab[k]).astype(BF)
-        sbuf[k, :, 0] = got[:, :cw].reshape(2 * ne, rows, cw)
-        sbuf[k, :, 1] = got[:, cw:].reshape(2 * ne, rows, cw)
-
-        @pl.when(is_in & (zz != out_z))
-        def _():
-            @pl.loop(0, ne)
-            def _(r):
-                b_copy(zz, h, lax.rem(own + r, ne), 1).start()
+        to = pl.ds(k * 2 * ne, 2 * ne)
+        sbuf[to, 0] = got[:, :cw].reshape(2 * ne, rows, cw)
+        sbuf[to, 1] = got[:, cw:].reshape(2 * ne, rows, cw)
 
         @pl.loop(1, ne)
         def _(r):
             b_copy(zz, h, lax.rem(own + r, ne), 0).start()
 
-        pair[:, row_at(d), col_at(zz, y, h)] = sbuf[k, own]
+        pair[:, row_at(d), col_at(zz, y, h)] = sbuf[k * 2 * ne + own]
+
+    def outward(i, first, count):
+        zz, h = place(i)
+
+        @pl.when(zz != out_z)
+        def _():
+            @pl.loop(first, first + count)
+            def _(r):
+                b_copy(zz, h, lax.rem(y * ndp + r, ne), 1).start()
 
     for i in range(nch):
         relay(i)
+
+    @pl.when(is_in)
+    def _():
+        for side in range(2):
+            for i in range(nch):
+                outward(i, side * ndp, ndp)
 
     for c in loads[npl + 2:]:
         c.wait()
@@ -408,16 +446,9 @@
     def c_copy(zz, h, e):
         k = zz * nch + h
         return remote(
-            gr.at[:, row_at(lax.rem(e, ndp)), col_at(zz, e // ndp, h)], rbuf.at[k, own],
-            cs.at[k * ne + e], cv.at[k * ne + own], lax.rem(e, ndp), z * 2 + e // ndp,
+            gr.at[:, row_at(lax.rem(e, ndp)), col_at(zz, e // ndp, h)], rbuf.at[k * ne + own],
+            cs.at[0], cv.at[k], lax.rem(e, ndp), z * 2 + e // ndp,
         )
-
-    def c_wait(zz, h, e):
-        k = zz * nch + h
-        remote(
-            gr.at[:, row_at(lax.rem(e, ndp)), col_at(zz, e // ndp, h)], rbuf.at[k, e],
-            cs.at[k * ne + e], cv.at[k * ne + e], d, other,
-        ).wait_recv()
 
     scale = DH ** (-0.5)
     to_exp2 = scale * 1.4426950408889634
@@ -425,19 +456,15 @@
     seen = iota((seq, seq), 0) <= iota((seq, seq), 1)
 
     def group(i):
-        zz, h = place(i)
+        zz, h = turn(i)
 
         @pl.when(is_in | (zz == z))
         def _():
-            @pl.loop(1, ne)
-            def _(r):
-                b_wait(zz, h, lax.rem(own + r, ne))
+            drain(rbuf.at[pl.ds(0, ne - 1)], bv.at[zz * nch + h])
 
         @pl.when(jnp.logical_not(is_in | (zz == z)))
         def _():
-            @pl.loop(0, ne)
-            def _(r):
-                b_wait(zz, h, r)
+            drain(rbuf.at[pl.ds(0, ne)], bv.at[zz * nch + h])
 
         ats, st, gt, va = [], [], [], []
         for yy in range(2):
@@ -465,46 +492,65 @@
         def _(r):
             c_copy(zz, h, lax.rem(own + r, ne)).start()
 
-        rbuf[zz * nch + h, own] = gr[:, row_at(d), col_at(zz, y, h)]
+        rbuf[(zz * nch + h) * ne + own] = gr[:, row_at(d), col_at(zz, y, h)]
 
     def u_copy(zz, h, dz, slot):
         k = zz * nch + h
         return remote(
-            ubuf.at[k], urec.at[slot * nch + h], us.at[k], uv.at[slot * nch + h], d, dz * 2 + y
+            ubuf.at[k], urec.at[slot * nch + h], us.at[0], uv.at[slot * nch + h], d, dz * 2 + y
         )
 
     def total(i):
-        zz, h = place(i)
+        zz, h = turn(i)
         k = zz * nch + h
 
-        @pl.loop(1, ne)
-        def _(r):
-            c_wait(zz, h, lax.rem(own + r, ne))
-
-        acc[k, :, :cw] = mm(sel_own, rbuf[k, :, 0].reshape(ne * rows, cw), 0, 0)
-        acc[k, :, cw:] = mm(sel_own, rbuf[k, :, 1].reshape(ne * rows, cw), 0, 0)
+        drain(rbuf.at[pl.ds(0, ne - 1)], cv.at[k])
+        at = pl.ds(k * ne, ne)
+        acc[k, :, :cw] = mm(sel_own, rbuf[at, 0].reshape(ne * rows, cw), 0, 0)
+        acc[k, :, cw:] = mm(sel_own, rbuf[at, 1].reshape(ne * rows, cw), 0, 0)
 
         @pl.when(is_in & (zz == out_z))
         def _():
             ubuf[k] = acc[k].astype(BF)
-            u_copy(zz, h, out_z, z).start()
+            u_copy(zz, h, zz, z).start()
 
         @pl.when(jnp.logical_not(is_in | (zz == z)))
         def _():
             ubuf[k] = acc[k].astype(BF)
             u_copy(zz, h, nxt, zz).start()
 
+    def combine(i):
+        zz, h = turn(i)
+        k = zz * nch + h
+        u_copy(zz, h, nxt, zz).wait_recv()
+        ubuf[k] = (acc[k] + urec[k].astype(F32)).astype(BF)
+        u_copy(zz, h, zz, jnp.where(zz == nxt, z + 2 * up, z)).start()
+
+    ahead = 2 * nch
+
+    @pl.when(is_in)
+    def _():
+        @pl.loop(nch, ahead)
+        def _(i):
+            relay(i)
+            outward(i, 0, ne)
+
     @pl.loop(0, steps)
     def _(i):
-        @pl.when(is_in & (i < steps - nch))
-        def _():
-            relay(i + nch)
-
         group(i)
 
+        @pl.when(is_in & (i < steps - ahead))
+        def _():
+            relay(i + ahead)
+            outward(i + ahead, 0, ne)
+
         @pl.when(i >= nch)
         def _():
             total(i - nch)
+
+        @pl.when(is_in & (i >= 3 * nch))
+        def _():
+            combine(i - 2 * nch)
 
     att_save = pltpu.make_async_copy(att_out, att_hbm, lsem.at[8])
     att_save.start()
@@ -513,20 +559,11 @@
     def _(i):
         total(i)
 
-    far = ((1, z + 2 * up), (2, z))
-
-    def u_far(off, slot, h):
-        return u_copy(z + up * off, h, z + up * off, slot)
-
     @pl.when(is_in)
     def _():
-        for off, slot in far:
-            for h in range(nch):
-                zz = z + up * off
-                k = zz * nch + h
-                u_copy(zz, h, zz, zz).wait_recv()
-                ubuf[k] = (acc[k] + urec[k].astype(F32)).astype(BF)
-                u_far(off, slot, h).start()
+        @pl.loop(steps - nch, steps)
+        def _(i):
+            combine(i)
 
     s1 = z + up * (1 - inner)
     s2 = z + up * (2 - 3 * inner)
@@ -534,15 +571,17 @@
     for h in range(nch):
         u_copy(z, h, nxt, s1).wait_recv()
         u_copy(z, h, nxt, s2).wait_recv()
-        t = acc[z * nch + h] + urec[s1 * nch + h].astype(F32) + urec[s2 * nch + h].astype(F32)
-        t = t.astype(BF)
+        k = z * nch + h
+        acc[k] = acc[k] + urec[s1 * nch + h].astype(F32) + urec[s2 * nch + h].astype(F32)
+
+        t = acc[k].astype(BF)
         tks.append(t[:, :cw])
         tvs.append(t[:, cw:])
     tk = jnp.concatenate(tks, axis=1)
     tv_ = jnp.concatenate(tvs, axis=1)
 
-    def term(slot, h):
-        at = pl.ds(pl.multiple_of(slot * width + h * cw, cw), cw)
+    def term(slot):
+        at = pl.ds(pl.multiple_of(slot * width, width), width)
         return mm(tk, kw_v[at, :], 1, 1) + mm(tv_, vw_v[at, :], 1, 1)
 
     def target(j):
@@ -550,18 +589,21 @@
 
     def y_copy(j, h):
         k = j * nch + h
-        return remote(ys.at[k], yr.at[k], hs.at[k], hv.at[k], d, other)
+        return remote(ys.at[k], yr.at[k], hs.at[0], hv.at[k], d, other)
 
     def z_copy(zz, h, dz, slot):
         k = zz * nch + h
         return remote(
-            zs.at[k], zr.at[slot * nch + h], es.at[k], ev.at[slot * nch + h], d, dz * 2 + y
+            zs.at[k], zr.at[slot * nch + h], es.at[0], ev.at[slot * nch + h], d, dz * 2 + y
         )
 
     for j in range(nz):
+        got = term(target(j) * 2 + (1 - y)).astype(BF)
         for h in range(nch):
-            ys[j * nch + h] = term(target(j) * 2 + (1 - y), h).astype(BF)
+            ys[j * nch + h] = got[:, h * cw : (h + 1) * cw]
             y_copy(j, h).start()
+    for j in range(nz):
+        zt[j] = term(target(j) * 2 + y)
 
     def route(j):
         zz = target(j)
@@ -576,9 +618,8 @@
         zz = target(j)
         for h in range(nch):
             k = zz * nch + h
-            mine = term(zz * 2 + y, h)
             y_copy(j, h).wait_recv()
-            mine = mine + yr[j * nch + h].astype(F32)
+            mine = zt[j, :, h * cw : (h + 1) * cw] + yr[j * nch + h].astype(F32)
             if j == nz - 1:
                 z_copy(z, h, nxt, s1).wait_recv()
                 z_copy(z, h, nxt, s2).wait_recv()
@@ -599,7 +640,9 @@
             dz, slot = route(j)
             z_copy(zz, h, dz, slot).start()
     tile = jnp.concatenate(tile, axis=1)
-    tile_out[...] = tile
+    tile_v[...] = tile
+    tile_save = pltpu.make_async_copy(tile_v, tile_hbm, lsem.at[11])
+    tile_save.start()
 
     prod = mm(p_v[...].reshape(spn, width), tile, 1, 1)
     prod = jnp.sum(jnp.where(same_row((spn, tp)), prod, 0.0).reshape(nsrc, rows, tp), axis=1)
@@ -612,7 +655,7 @@
 
     def w_copy(k):
         to = lax.rem(me + k, n)
-        return remote(wp, wbuf.at[me], ws.at[k], wv.at[k], to // nmp, lax.rem(to, nmp))
+        return remote(wp, wbuf.at[me], ws.at[0], wv.at[0], to // nmp, lax.rem(to, nmp))
 
     @pl.loop(1, n)
     def _(k):
@@ -620,61 +663,30 @@
 
     w_save.wait()
     att_save.wait()
-
-    for h in range(nch):
-        g_copy(z, h, nxt).wait_send()
-        f_copy(z, h, y).wait_send()
-        t_copy(z, h).wait_send()
-
-    @pl.loop(nch, steps)
-    def _(i):
-        zz, h = place(i)
-        f_copy(zz, h, y).wait_send()
-
-        @pl.when(is_in)
-        def _():
-            g_copy(zz, h, nxt).wait_send()
-
-        @pl.when(is_in & (zz == out_z))
-        def _():
-            t_copy(zz, h).wait_send()
-
-        u_copy(zz, h, nxt, s1).wait_send()
+    tile_save.wait()
+
+    moved = steps - nch
+    drain(mixed.at[pl.ds(0, nz)], fs.at[0])
+    drain(ids_buf.at[pl.ds(0, ndp - 1)], js.at[0])
+    drain(rbuf.at[pl.ds(0, steps * (ne - 1))], cs.at[0])
+    drain(ubuf.at[pl.ds(0, moved)], us.at[0])
+    drain(ys, hs.at[0])
+    drain(zs.at[pl.ds(0, moved)], es.at[0])
 
     @pl.when(is_in)
     def _():
-        for h in range(nch):
-            g2_copy(h).wait_send()
-
-    for j in range(nz):
-        for h in range(nch):
-            y_copy(j, h).wait_send()
-            if j < nz - 1:
-                z_copy(target(j), h, nxt, s1).wait_send()
-
-    @pl.loop(0, steps)
-    def _(i):
-        zz, h = place(i)
-
-        @pl.loop(1, ne)
-        def _(r):
-            c_copy(zz, h, lax.rem(own + r, ne)).wait_send()
-
-        @pl.when(is_in | (zz == z))
-        def _():
-            @pl.loop(1, ne)
-            def _(r):
-                b_copy(zz, h, lax.rem(own + r, ne), 0).wait_send()
-
-        @pl.when(is_in & (zz != out_z))
-        def _():
-            @pl.loop(0, ne)
-            def _(r):
-                b_copy(zz, h, r, 1).wait_send()
-
-    @pl.loop(1, n)
-    def _(k):
-        w_copy(k).wait()
+        drain(mixed.at[pl.ds(0, nz)], gs.at[0])
+        drain(tab.at[pl.ds(0, 2 * nch)], ts.at[0])
+        drain(sbuf.at[pl.ds(0, steps * (ne - 1) + moved * ne)], bs.at[0])
+
+    @pl.when(jnp.logical_not(is_in))
+    def _():
+        drain(mixed.at[pl.ds(0, nz // 2)], gs.at[0])
+        drain(tab.at[pl.ds(0, nch)], ts.at[0])
+        drain(sbuf.at[pl.ds(0, nch * (ne - 1))], bs.at[0])
+
+    drain(wbuf.at[pl.ds(0, n - 1)], ws.at[0])
+    drain(wbuf.at[pl.ds(0, n - 1)], wv.at[0])
 
     wg = jnp.sum(wbuf[...], axis=0)
     lg_out[...] = mix * (wg - jnp.sum(mix * wg, axis=1, keepdims=True))
@@ -712,9 +724,12 @@
             jax.ShapeDtypeStruct((ntask, nsrc), F32),
             jax.ShapeDtypeStruct((tp, spn), BF),
         ),
-        in_specs=[vmem, pl.BlockSpec(memory_space=pltpu.SMEM)] + [hbm] * 7,
-        out_specs=(hbm, vmem, vmem, hbm),
+        in_specs=[hbm] * 9,
+        out_specs=(hbm, hbm, vmem, hbm),
         scratch_shapes=[
+            pltpu.VMEM((ntask, nsrc), F32),
+            pltpu.SMEM((ge,), jnp.int32),
+            pltpu.VMEM((tp, width), BF),
             pltpu.VMEM((seq, full), BF),
             pltpu.VMEM((tp, spn), BF),
             pltpu.VMEM((nsrc, rows, width), BF),
@@ -728,10 +743,10 @@
             pltpu.VMEM((ge, tp), F32),
             pltpu.VMEM((ndp, ge, tp), F32),
             pltpu.VMEM((st, tp, 2 * cw), BF),
-            pltpu.VMEM((st, 2 * ne, 2, rows, cw), BF),
+            pltpu.VMEM((st * 2 * ne, 2, rows, cw), BF),
             pltpu.VMEM((2, ptok, full), BF),
             pltpu.VMEM((2, ptok, full), BF),
-            pltpu.VMEM((st, ne, 2, rows, cw), BF),
+            pltpu.VMEM((st * ne, 2, rows, cw), BF),
             pltpu.VMEM((st, tp, 2 * cw), F32),
             pltpu.VMEM((st, tp, 2 * cw), BF),
             pltpu.VMEM((st, tp, 2 * cw), BF),
@@ -739,15 +754,14 @@
             pltpu.VMEM((st, tp, cw), BF),
             pltpu.VMEM((st, tp, cw), BF),
             pltpu.VMEM((st, tp, cw), BF),
+            pltpu.VMEM((nz, tp, width), F32),
             pltpu.VMEM((ntask, nsrc), F32),
             pltpu.VMEM((n, ntask, nsrc), F32),
-            dma((13,)),
-            dma((st + nch,)), dma((st,)), dma((st,)), dma((st,)),
-            dma((ndp,)), dma((ndp,)),
-            dma((st,)), dma((st,)),
-            dma((st * 2 * ne,)), dma((st * ne,)), dma((st * ne,)), dma((st * ne,)),
-            dma((st,)), dma((st,)), dma((st,)), dma((st,)), dma((st,)), dma((st,)),
-            dma((n,)), dma((n,)),
+            dma((12,)),
+            dma((1,)), dma((st,)), dma((1,)), dma((st,)), dma((1,)), dma((1,)),
+            dma((1,)), dma((st,)), dma((1,)), dma((st,)), dma((1,)), dma((st,)),
+            dma((1,)), dma((st,)), dma((1,)), dma((st,)), dma((1,)), dma((st,)),
+            dma((1,)), dma((1,)),
         ],
         compiler_params=pltpu.CompilerParams(
             collective_id=0, has_side_effects=True, vmem_limit_bytes=60 * 2**20

time: 99.2 us -> 89.8 us (0.905)
  Pallas kernels: 98.3 us -> 89 us
    pallas_call x1, Pallas kernels: 94.4 us -> 85.1 us  [per_device(): pl.pallas_call(functools.partial(chain_kernel, ndp, nmp, nch), out_shape=...]
where the time goes in v2:
time: 89.8 us; the launch traced here: 89.7 us
  Pallas kernels  89 us (99%)
    pallas_call x1, Pallas kernels, per_device(): pl.pallas_call(functools.partial(chain_kernel, ndp, nmp, nch), out_shape=...  85.1 us
    pallas_call x1, Pallas kernels, per_device(): pl.pallas_call(source_kernel, grid=(steps,), out_shape=(jax.ShapeDtypeStr...  3.95 us

profile of v2, /device:TPU:0, one launch (start us, length us, event | category | flops | bytes accessed | tf_op | source)
XLA Modules:
  0.0 89.7 jit_solution(1145690802286229332)
XLA Ops:
  0.6 85.1 %chain.1 = (bf16[128,4096]{1,0:T(8,128)(2,1)}, bf16[128,512]{1,0:T(8,128)(2,1)}, f32[8,128]{1,0:T(8,128)}, bf16[128,2048]{1,0:T(8,128)(2,1)}) custom-call(f32[8,128]{1,0:T(8,128)} %lg_hbm.1, s32[8]{0:T(128)} %ids_hbm.1, bf16[128,64,512]{2,1,0:T(8,128)(2,1)} %sp_hbm.1, bf16[4096,512]{1,0:T(8,128)(2,1)} %kw_hbm.1, bf16[4096,512]{1,0:T(8,128)(2,1)} %vw_hbm.1, ...), custom_call_target="tpu_custom_call" | custom-call | tf_op jit(solution)/shard_map/chain/pallas_call | solution.py:719
  85.7 3.9 %source_grad.1 = (f32[128,16,512]{2,1,0:T(8,128)}, bf16[128,4096]{1,0:T(8,128)(2,1)}, f32[8,128]{1,0:T(8,128)}) custom-call(bf16[128,2048]{1,0:T(8,128)(2,1)} %get-tuple-element.10.w_ref, bf16[128,512]{1,0:T(8,128)(2,1)} %get-tuple-element.11.tile_ref, bf16[128,4096]{1,0:T(8,128)(2,1)} %get-tuple-element.12.att_ref, f32[8,128]{1,0:T(8,128)} %get-tuple-element.13.lg_ref), custom_call_target="tpu_custom_call" | custom-call | tf_op jit(solution)/shard_map/source_grad/pallas_call | solution.py:776

commit v3 on v2

--- a/solution.py
+++ b/solution.py
@@ -159,8 +159,8 @@
     lg_hbm, ids_hbm, sp_hbm, kw_hbm, vw_hbm, q_hbm, k_hbm, v_hbm, c_hbm,
     att_hbm, tile_hbm, lg_out, w_hbm,
     logits, ids_in, tile_v, att_out, w_out, p_v, kw_v, vw_v, q_v, k_v, v_v, c_v,
-    mixed, ids_own, ids_buf, tab, sbuf, pair, gr, rbuf, acc, ubuf, urec, ys, yr, zs, zr, zt, wp, wbuf,
-    lsem, gs, gv, fs, fv, js, jv, ts, tv, bs, bv, cs, cv, us, uv, hs, hv, es, ev, ws, wv,
+    mixed, ids_own, ids_buf, tab, sbuf, pair, gr, rbuf, acc, ubuf, urec, ys, yr, zs, zr, zt, xr, wp, wbuf,
+    lsem, gs, gv, fs, fv, js, jv, ts, tv, bs, bv, cs, cv, us, uv, hs, hv, es, ev, xv, ws, wv,
 ):
     n = ndp * nmp
     nz = nmp // 2
@@ -597,25 +597,74 @@
             zs.at[k], zr.at[slot * nch + h], es.at[0], ev.at[slot * nch + h], d, dz * 2 + y
         )
 
-    for j in range(nz):
-        got = term(target(j) * 2 + (1 - y)).astype(BF)
+    def cut(a, h):
+        return a[:, h * cw : (h + 1) * cw]
+
+    def x_copy(h):
+        k = 2 * nch + h
+        return remote(ys.at[k], xr.at[h], hs.at[0], xv.at[h], d, nxt * 2 + y)
+
+    for j in (0, 2, 1, 3):
+        got = term(target(j) * 2 + (1 - y))
+        if j == 3:
+            zt[j] = got
         for h in range(nch):
-            ys[j * nch + h] = got[:, h * cw : (h + 1) * cw]
-            y_copy(j, h).start()
-    for j in range(nz):
+            if j < 3:
+                ys[j * nch + h] = cut(got, h).astype(BF)
+            if j == 2:
+                @pl.when(is_in)
+                def _():
+                    y_copy(j, h).start()
+
+                @pl.when(jnp.logical_not(is_in))
+                def _():
+                    x_copy(h).start()
+            elif j < 2:
+                y_copy(j, h).start()
+
+    @pl.when(jnp.logical_not(is_in))
+    def _():
+        for h in range(nch):
+            ys[3 * nch + h] = zt[3, :, h * cw : (h + 1) * cw].astype(BF)
+            y_copy(3, h).start()
+        got = term(nxt * 2 + y)
+        for h in range(nch):
+            zs[nxt * nch + h] = cut(got, h).astype(BF)
+
+    for j in (0, 1):
         zt[j] = term(target(j) * 2 + y)
+
+    @pl.when(is_in)
+    def _():
+        got = term(out_z * 2 + y)
+        for h in range(nch):
+            k = out_z * nch + h
+            y_copy(2, h).wait_recv()
+            zs[k] = (cut(got, h) + yr[2 * nch + h].astype(F32)).astype(BF)
+            z_copy(out_z, h, out_z, z).start()
+        for h in range(nch):
+            x_copy(h).wait_recv()
+            k = 3 * nch + h
+            ys[k] = (zt[3, :, h * cw : (h + 1) * cw] + xr[h].astype(F32)).astype(BF)
+            y_copy(3, h).start()
+
+    zt[3] = term(z * 2 + y)
 
     def route(j):
         zz = target(j)
         if j == 0:
             return jnp.where(is_in, zz, nxt), jnp.where(is_in, z, zz)
-        if j == 1:
-            return jnp.where(is_in, zz, nxt), jnp.where(is_in, z + 2 * up, zz)
-        return jnp.where(is_in, out_z, nxt), jnp.where(is_in, z, zz)
-
-    tile = []
-    for j in range(nz):
+        return jnp.where(is_in, zz, nxt), jnp.where(is_in, z + 2 * up, zz)
+
+    tile, sums = [], []
+    for j in (0, 1, 3):
         zz = target(j)
+        if j == 3:
+            @pl.when(jnp.logical_not(is_in))
+            def _():
+                for h in range(nch):
+                    z_copy(nxt, h, nxt, nxt).start()
+
         for h in range(nch):
             k = zz * nch + h
             y_copy(j, h).wait_recv()
@@ -624,19 +673,20 @@
                 z_copy(z, h, nxt, s1).wait_recv()
                 z_copy(z, h, nxt, s2).wait_recv()
                 mine = mine + zr[s1 * nch + h].astype(F32) + zr[s2 * nch + h].astype(F32)
-                tile.append(mine.astype(BF))
+                piece = mine.astype(BF)
+                tile.append(piece)
+                half = p_v[:, :, h * cw : (h + 1) * cw].reshape(spn, cw)
+                got = jnp.where(same_row((spn, tp)), mm(half, piece, 1, 1), 0.0)
+                sums.append(jnp.sum(got.reshape(nsrc, rows, tp), axis=1))
                 continue
-            if j < 2:
-                acc[k, :, :cw] = mine
-
-                @pl.when(is_in)
-                def _():
-                    z_copy(zz, h, zz, zz).wait_recv()
-                    acc[k, :, :cw] = acc[k, :, :cw] + zr[k].astype(F32)
-
-                zs[k] = acc[k, :, :cw].astype(BF)
-            else:
-                zs[k] = mine.astype(BF)
+            acc[k, :, :cw] = mine
+
+            @pl.when(is_in)
+            def _():
+                z_copy(zz, h, zz, zz).wait_recv()
+                acc[k, :, :cw] = acc[k, :, :cw] + zr[k].astype(F32)
+
+            zs[k] = acc[k, :, :cw].astype(BF)
             dz, slot = route(j)
             z_copy(zz, h, dz, slot).start()
     tile = jnp.concatenate(tile, axis=1)
@@ -644,8 +694,7 @@
     tile_save = pltpu.make_async_copy(tile_v, tile_hbm, lsem.at[11])
     tile_save.start()
 
-    prod = mm(p_v[...].reshape(spn, width), tile, 1, 1)
-    prod = jnp.sum(jnp.where(same_row((spn, tp)), prod, 0.0).reshape(nsrc, rows, tp), axis=1)
+    prod = sum(sums[1:], sums[0])
     fold = (
         outer(iota((ntask, tp), 1)) == iota((ntask, tp), 0)
     )
@@ -692,11 +741,41 @@
     lg_out[...] = mix * (wg - jnp.sum(mix * wg, axis=1, keepdims=True))
 
 
-def source_kernel(w_ref, tile_ref, att_ref, lg_ref, out_ref, att_out, lg_out):
-    att_out[...] = att_ref[...]
-    lg_out[...] = lg_ref[...]
-    got = mm(w_ref[...], tile_ref[...], 0, 0)
-    out_ref[...] = got.reshape(out_ref.shape)
+def source_kernel(
+    parts, w_hbm, tile_hbm, att_hbm, lg_hbm, out_hbm, att_out, lg_out,
+    w_v, tile_v, att_v, lg_v, out_v, isem, osem,
+):
+    nsrc, rows, width = out_hbm.shape
+    cols = nsrc * rows // parts
+    part = nsrc // parts
+    tile_in = pltpu.make_async_copy(tile_hbm, tile_v, isem.at[parts])
+    tile_in.start()
+    ins, outs = [], []
+    for i in range(parts):
+        at = pl.ds(i * cols, cols)
+        ins.append(pltpu.make_async_copy(w_hbm.at[:, at], w_v.at[:, at], isem.at[i]))
+        ins[i].start()
+    att_in = pltpu.make_async_copy(att_hbm, att_v, isem.at[parts + 1])
+    lg_in = pltpu.make_async_copy(lg_hbm, lg_v, isem.at[parts + 2])
+    att_in.start()
+    lg_in.start()
+    tile_in.wait()
+    for i in range(parts):
+        ins[i].wait()
+        at = pl.ds(i * part, part)
+        got = mm(w_v[:, i * cols : (i + 1) * cols], tile_v[...], 0, 0)
+        out_v[at] = got.reshape(part, rows, width)
+        outs.append(pltpu.make_async_copy(out_v.at[at], out_hbm.at[at], osem.at[i]))
+        outs[i].start()
+        if i == 0:
+            att_in.wait()
+            outs_att = pltpu.make_async_copy(att_v, att_out, osem.at[parts])
+            outs_att.start()
+            lg_in.wait()
+            outs_lg = pltpu.make_async_copy(lg_v, lg_out, osem.at[parts + 1])
+            outs_lg.start()
+    for c in outs + [outs_att, outs_lg]:
+        c.wait()
 
 
 def per_device(ndp, nmp, *args):
@@ -755,13 +834,14 @@
             pltpu.VMEM((st, tp, cw), BF),
             pltpu.VMEM((st, tp, cw), BF),
             pltpu.VMEM((nz, tp, width), F32),
+            pltpu.VMEM((nch, tp, cw), BF),
             pltpu.VMEM((ntask, nsrc), F32),
             pltpu.VMEM((n, ntask, nsrc), F32),
             dma((12,)),
             dma((1,)), dma((st,)), dma((1,)), dma((st,)), dma((1,)), dma((1,)),
             dma((1,)), dma((st,)), dma((1,)), dma((st,)), dma((1,)), dma((st,)),
             dma((1,)), dma((st,)), dma((1,)), dma((st,)), dma((1,)), dma((st,)),
-            dma((1,)), dma((1,)),
+            dma((nch,)), dma((1,)), dma((1,)),
         ],
         compiler_params=pltpu.CompilerParams(
             collective_id=0, has_side_effects=True, vmem_limit_bytes=60 * 2**20
@@ -772,26 +852,25 @@
         queries.reshape(seq, full), keys.reshape(seq, full),
         values.reshape(seq, full), cotangent.reshape(seq, full),
     )
-    steps = 2
+    parts = 4
     source_grad, attended, logits_grad = pl.pallas_call(
-        source_kernel,
-        grid=(steps,),
+        functools.partial(source_kernel, parts),
         out_shape=(
             jax.ShapeDtypeStruct((nsrc, rows, width), F32),
             jax.ShapeDtypeStruct((seq, full), BF),
             jax.ShapeDtypeStruct((ntask, nsrc), F32),
         ),
-        in_specs=[
-            pl.BlockSpec((tp, spn // steps), lambda i: (0, i)),
-            pl.BlockSpec((tp, width), lambda i: (0, 0)),
-            pl.BlockSpec((seq // steps, full), lambda i: (i, 0)),
-            pl.BlockSpec((ntask, nsrc), lambda i: (0, 0)),
+        in_specs=[hbm] * 4,
+        out_specs=(hbm, hbm, hbm),
+        scratch_shapes=[
+            pltpu.VMEM((tp, spn), BF),
+            pltpu.VMEM((tp, width), BF),
+            pltpu.VMEM((seq, full), BF),
+            pltpu.VMEM((ntask, nsrc), F32),
+            pltpu.VMEM((nsrc, rows, width), F32),
+            dma((parts + 3,)), dma((parts + 2,)),
         ],
-        out_specs=(
-            pl.BlockSpec((nsrc // steps, rows, width), lambda i: (i, 0, 0)),
-            pl.BlockSpec((seq // steps, full), lambda i: (i, 0)),
-            pl.BlockSpec((ntask, nsrc), lambda i: (0, 0)),
-        ),
+        compiler_params=pltpu.CompilerParams(vmem_limit_bytes=60 * 2**20),
         name="source_grad",
     )(w_big, tile, attended, logits_grad)
     return (attended.reshape(queries.shape), source_grad, logits_grad)

time: 89.8 us -> 87.4 us (0.973)
  Pallas kernels: 89 us -> 86.6 us
    pallas_call x1, Pallas kernels: 85.1 us -> 82.8 us  [per_device(): pl.pallas_call(functools.partial(chain_kernel, ndp, nmp, nch), out_shape=...]
where the time goes in v3:
time: 87.4 us; the launch traced here: 87.2 us
  Pallas kernels  86.6 us (99%)
    pallas_call x1, Pallas kernels, per_device(): pl.pallas_call(functools.partial(chain_kernel, ndp, nmp, nch), out_shape=...  82.8 us
    pallas_call x1, Pallas kernels, per_device(): pl.pallas_call(functools.partial(source_kernel, parts), out_shape=(jax.Sh...  3.75 us

profile of v3, /device:TPU:0, one launch (start us, length us, event | category | flops | bytes accessed | tf_op | source)
XLA Modules:
  0.0 87.2 jit_solution(12289567327470908645)
XLA Ops:
  0.6 82.8 %chain.1 = (bf16[128,4096]{1,0:T(8,128)(2,1)}, bf16[128,512]{1,0:T(8,128)(2,1)}, f32[8,128]{1,0:T(8,128)}, bf16[128,2048]{1,0:T(8,128)(2,1)}) custom-call(f32[8,128]{1,0:T(8,128)} %lg_hbm.1, s32[8]{0:T(128)} %ids_hbm.1, bf16[128,64,512]{2,1,0:T(8,128)(2,1)} %sp_hbm.1, bf16[4096,512]{1,0:T(8,128)(2,1)} %kw_hbm.1, bf16[4096,512]{1,0:T(8,128)(2,1)} %vw_hbm.1, ...), custom_call_target="tpu_custom_call" | custom-call | tf_op jit(solution)/shard_map/chain/pallas_call | solution.py:798
  83.5 3.8 %source_grad.1 = (f32[128,16,512]{2,1,0:T(8,128)}, bf16[128,4096]{1,0:T(8,128)(2,1)}, f32[8,128]{1,0:T(8,128)}) custom-call(bf16[128,2048]{1,0:T(8,128)(2,1)} %get-tuple-element.10.w_hbm, bf16[128,512]{1,0:T(8,128)(2,1)} %get-tuple-element.11.tile_hbm, bf16[128,4096]{1,0:T(8,128)(2,1)} %get-tuple-element.12.att_hbm, f32[8,128]{1,0:T(8,128)} %get-tuple-element.13.lg_hbm), custom_call_target="tpu_custom_call" | custom-call | tf_op jit(solution)/shard_map/source_grad/pallas_call | solution.py:856
